TPU v7x, 128 devices: a whole 4x4x4 slice. The times are simulated.
128 devices in a mesh: lat: 4 (over y), lon: 16 (over z, x), mem: 2 (over core).
Axes of the slice: x: 4, y: 4, z: 4, core: 2. Of those that a mesh axis runs over, the one named last changes fastest.
Arguments:
- anomalies: bfloat16 [24, 16, 1440, 512], P('mem', None, 'lon', 'lat'), may hold values from -6 to 6
- taper: float32 [16, 1440, 512], P('lon', 'lat'), may hold values from 0.5 to 8
- obs_row: int32 [256, 2048], P('lat', 'lon'), may hold values from 0 to 511, as said below
- obs_col: int32 [256, 2048], P('lat', 'lon'), may hold values from 0 to 1439, as said below
- obs_level: int32 [256, 2048], P('lat', 'lon'), may hold values from 0 to 15
- obs_value: float32 [256, 2048], P('lat', 'lon'), may hold values from -18 to 18
Outputs:
- increment: float32 [16, 1440, 512], P(None, 'lon', 'lat')
Inputs may be any that keep to these rules, and one draw needn't show every extreme that they name: `obs_row`: the entry in row i lies in latitude rows (i // 64) * 128 to (i // 64 + 1) * 128 - 1, drawn evenly there. `obs_col`: the entry in column j lies in longitude columns (j // 128) * 90 to (j // 128 + 1) * 90 - 1, drawn evenly there.
All inputs are finite; a program needn't handle non-finite values.
Results may differ from a plain program's by a relative error of at most 0.0066.
Values may be sent and summed in bfloat16 or wider, within the bound.
No kernel may reach another device: no remote copies, remote signals or barrier semaphores. Data moves between devices by JAX's collectives and lax.ppermute only.
A program may use at most 128 MiB of HBM per device.

v0:
```python
import math

import jax
import jax.numpy as jnp
from jax import lax
from jax.experimental import pallas as pl
from jax.experimental.pallas import tpu as pltpu
from jax.sharding import PartitionSpec as P

BF = jnp.bfloat16
F32 = jnp.float32
LL = ("lat", "lon")
SWAP = [(0, 1), (1, 0)]


def vspec():
    return pl.BlockSpec(memory_space=pltpu.VMEM)


def sspec():
    return pl.BlockSpec(memory_space=pltpu.SMEM)


def params(mib):
    return pltpu.CompilerParams(vmem_limit_bytes=mib * 1024 * 1024)


def over_all(x):
    return lax.all_to_all(x, LL, split_axis=0, concat_axis=0, tiled=True)


def spread_kernel(place, row_ref, col_ref, level_ref, value_ref, out_ref, acc, *, half, levels, copies):
    mem = place[0]
    slots = levels * half
    acc[...] = jnp.zeros_like(acc)
    slot_ids = lax.broadcasted_iota(jnp.int32, (slots, 128), 0)
    row_ids = lax.broadcasted_iota(jnp.int32, (128, 128), 0)

    def add_group(g, carry):
        rows = pl.ds(pl.multiple_of(g * 8, 8), 8)
        within = col_ref[rows, :] - place[2] - mem * half
        inside = (within >= 0) & (within < half)
        keys = jnp.where(inside, level_ref[rows, :] * half + within, -1)
        lat_row = row_ref[rows, :] - place[1]
        value = value_ref[rows, :]
        high = value.astype(BF).astype(F32)
        middle = value - high
        left = []
        right = []
        for r in range(8):
            hit = slot_ids == keys[r : r + 1, :]
            left.append(jnp.where(hit, 1.0, 0.0).astype(BF))
            row_hit = row_ids == lat_row[r : r + 1, :]
            top = jnp.where(row_hit, high[r : r + 1, :], 0.0)
            low = jnp.where(row_hit, middle[r : r + 1, :], 0.0)
            right.append(jnp.concatenate([top, low], axis=0).astype(BF))
        acc[...] += lax.dot_general(
            jnp.concatenate(left, axis=1),
            jnp.concatenate(right, axis=1),
            (((1,), (1,)), ((), ())),
            preferred_element_type=F32,
        )
        return carry

    lax.fori_loop(0, row_ref.shape[0] // 8, add_group, 0)
    summed = (acc[:, :128] + acc[:, 128:]).astype(BF).reshape(levels, half, 128)
    for copy in range(copies):
        out_ref[copy] = summed


def spread(place, obs_row, obs_col, obs_level, obs_value, half, levels, copies):
    return pl.pallas_call(
        lambda *refs: spread_kernel(*refs, half=half, levels=levels, copies=copies),
        out_shape=jax.ShapeDtypeStruct((copies, levels, half, 128), BF),
        in_specs=[sspec()] + [vspec()] * 4,
        out_specs=vspec(),
        scratch_shapes=[pltpu.VMEM((levels * half, 256), F32)],
        compiler_params=params(24),
        name="spread",
    )(place, obs_row, obs_col, obs_level, obs_value)


def basis_kernel(lon_ref, lon_t_ref, lat_ref, lat_t_ref, *, cols, blocks, padded):
    total = cols * blocks
    half = total // 2
    tiles = lon_ref.shape[1] // 128
    lanes = lax.broadcasted_iota(jnp.int32, (padded, 128), 1)

    def angles(product):
        turns = (product.astype(F32) * (1.0 / total)).astype(jnp.int32)
        return (product - turns * total).astype(F32) * (2.0 * math.pi / total)

    def lon_rows(j, carry):
        within = lax.broadcasted_iota(jnp.int32, (padded, 128), 0)
        x = within + cols * j
        fine = angles(x * lanes)
        coarse = angles(x * lax.rem(lanes * 128, total))
        fine_cos = jnp.cos(fine)
        fine_sin = jnp.sin(fine)
        scale = jnp.where(within < cols, math.sqrt(2.0 / total), 0.0)
        coarse_cos = jnp.cos(coarse) * scale
        coarse_sin = jnp.sin(coarse) * scale
        sign = jnp.where((x & 1) == 0, 1.0, -1.0)
        rows = pl.ds(pl.multiple_of(j * padded, padded), padded)
        for t in range(tiles):
            c = lanes + 128 * t
            cos_t = coarse_cos[:, t : t + 1]
            sin_t = coarse_sin[:, t : t + 1]
            parts = []
            if 128 * t <= half:
                parts.append(fine_cos * cos_t - fine_sin * sin_t)
            if 128 * t + 127 > half:
                parts.append((fine_sin * cos_t + fine_cos * sin_t) * sign)
            value = parts[0] if len(parts) == 1 else jnp.where(c <= half, parts[0], parts[1])
            if t == 0 or 128 * t <= half < 128 * t + 128:
                value = jnp.where((c == 0) | (c == half), value * math.sqrt(0.5), value)
            if 128 * t + 127 >= total:
                value = jnp.where(c < total, value, 0.0)
            lon_ref[rows, 128 * t : 128 * t + 128] = value.astype(BF)
        return carry

    lax.fori_loop(0, blocks, lon_rows, 0)
    for t in range(tiles):
        strip = lon_ref[:, 128 * t : 128 * t + 128].astype(F32)
        lon_t_ref[128 * t : 128 * t + 128, :] = strip.T.astype(BF)

    length = lat_ref.shape[0]
    step = 64

    def lat_rows(i, carry):
        shape = (step, length)
        down = lax.broadcasted_iota(jnp.int32, shape, 0) + step * i
        across = lax.broadcasted_iota(jnp.int32, shape, 1)
        rows = pl.ds(pl.multiple_of(i * step, step), step)
        for grid, mode, ref in ((down, across, lat_ref), (across, down, lat_t_ref)):
            phase = (mode * (2 * grid + 1)) & (4 * length - 1)
            angle = phase.astype(F32) * (math.pi / (2.0 * length))
            scale = jnp.where(mode == 0, 1.0 / math.sqrt(length), math.sqrt(2.0 / length))
            ref[rows, :] = (jnp.cos(angle) * scale).astype(BF)
        return carry

    lax.fori_loop(0, length // step, lat_rows, 0)


def bases(cols, blocks, padded, lat_total):
    wide = padded * blocks
    return pl.pallas_call(
        lambda *refs: basis_kernel(*refs, cols=cols, blocks=blocks, padded=padded),
        out_shape=(
            jax.ShapeDtypeStruct((wide, wide), BF),
            jax.ShapeDtypeStruct((wide, wide), BF),
            jax.ShapeDtypeStruct((lat_total, lat_total), BF),
            jax.ShapeDtypeStruct((lat_total, lat_total), BF),
        ),
        out_specs=(vspec(),) * 4,
        compiler_params=params(40),
        name="bases",
    )()


def member_kernel(*refs, first, final, cols, blocks, bands, padded, coefs):
    place, field, innov_own, innov_other, taper_own, taper_other = refs[:6]
    lon_ref, lon_t_ref, lat_ref, lat_t_ref = refs[6:10]
    rest = list(refs[10:])
    so_far = None if first else rest.pop(0)
    if final:
        own_out, other_out = rest[:2]
        rest = rest[2:]
        innov, taper, weighted, inverse, acc = rest
    else:
        acc = rest.pop(0)
        innov, taper, weighted, inverse = rest
    mem = place[0]
    half = padded // 2
    wide = padded * blocks
    own_rows = pl.ds(pl.multiple_of(mem * half, half), half)
    other_rows = pl.ds(pl.multiple_of((1 - mem) * half, half), half)
    innov[:, own_rows, :] = innov_own[...]
    innov[:, other_rows, :] = innov_other[...]
    taper[mem] = taper_own[...]
    taper[1 - mem] = taper_other[...]
    weighted[...] = jnp.zeros_like(weighted)
    inverse[coefs:, :] = jnp.zeros((wide - coefs, inverse.shape[1]), BF)

    def weigh(j, carry):
        rows = pl.ds(pl.multiple_of(j * padded, padded), cols)
        for a in range(bands):
            product = field[a * blocks + j] * innov[a * blocks + j, :cols, :]
            weighted[rows, 128 * a : 128 * a + 128] = product
        return carry

    lax.fori_loop(0, blocks, weigh, 0)
    step = coefs // 3

    def spectral(i, carry):
        rows = pl.ds(pl.multiple_of(i * step, 16), step)
        zonal = jnp.dot(lon_t_ref[rows, :], weighted[...], preferred_element_type=F32).astype(BF)
        spectrum = jnp.dot(zonal, lat_ref[...], preferred_element_type=F32)
        weights = jnp.concatenate([taper[0, rows, :], taper[1, rows, :]], axis=1).astype(F32)
        tapered = (spectrum * weights).astype(BF)
        inverse[rows, :] = jnp.dot(tapered, lat_t_ref[...], preferred_element_type=F32).astype(BF)
        return carry

    lax.fori_loop(0, 3, spectral, 0)
    group = 4

    def gridded(i, carry):
        rows = pl.ds(pl.multiple_of(i * group * padded, padded), group * padded)
        localized = jnp.dot(lon_ref[rows, :], inverse[...], preferred_element_type=F32)
        for g in range(group):
            j = i * group + g
            for a in range(bands):
                spot = a * blocks + j
                piece = localized[g * padded : g * padded + cols, 128 * a : 128 * a + 128]
                piece = piece * field[spot].astype(F32)
                if not first:
                    piece = piece + so_far[spot, :cols, :]
                acc[spot, :cols, :] = piece
        return carry

    lax.fori_loop(0, blocks // group, gridded, 0)
    if final:
        own_out[...] = acc[:, own_rows, :]
        other_out[...] = acc[:, other_rows, :].astype(BF)


def member(place, field, innov, taper, tables, so_far, final, dims):
    cols, blocks, bands, padded, coefs, lat_total = dims
    spots = bands * blocks
    half = padded // 2
    wide = padded * blocks
    first = so_far is None
    operands = [place, field, *innov, *taper, *tables] + ([] if first else [so_far])
    scratch = [
        pltpu.VMEM((spots, padded, 128), BF),
        pltpu.VMEM((2, coefs, lat_total // 2), BF),
        pltpu.VMEM((wide, lat_total), BF),
        pltpu.VMEM((wide, lat_total), BF),
    ]
    if final:
        out_shape = (
            jax.ShapeDtypeStruct((spots, half, 128), F32),
            jax.ShapeDtypeStruct((spots, half, 128), BF),
        )
        out_specs = (vspec(), vspec())
        scratch.append(pltpu.VMEM((spots, padded, 128), F32))
    else:
        out_shape = jax.ShapeDtypeStruct((spots, padded, 128), F32)
        out_specs = vspec()
    return pl.pallas_call(
        lambda *refs: member_kernel(
            *refs, first=first, final=final, cols=cols, blocks=blocks, bands=bands, padded=padded, coefs=coefs
        ),
        out_shape=out_shape,
        in_specs=[sspec()] + [vspec()] * (len(operands) - 1),
        out_specs=out_specs,
        scratch_shapes=scratch,
        compiler_params=params(48),
        name="member",
    )(*operands)


def local(anomalies, taper, obs_row, obs_col, obs_level, obs_value):
    members, levels, cols, lat_rows = anomalies.shape
    bands = lax.axis_size("lat")
    blocks = lax.axis_size("lon")
    mem = lax.axis_index("mem")
    coefs = cols * blocks
    lat_total = lat_rows * bands
    padded = -(-cols // 32) * 32
    half = padded // 2
    ensemble = members * lax.axis_size("mem")
    place = jnp.stack([mem, lax.axis_index("lat") * lat_rows, lax.axis_index("lon") * cols]).astype(jnp.int32)

    chunks = [
        over_all(anomalies[i : i + bands].reshape(bands * levels, cols, lat_rows))
        for i in range(0, members, bands)
    ]

    innovation = spread(place, obs_row, obs_col, obs_level, obs_value, half, levels, bands)
    innov_own = over_all(innovation.reshape(bands * levels, half, lat_rows))
    innov_other = lax.ppermute(innov_own, "mem", SWAP)

    n_half = lat_total // 2
    taper_own = lax.dynamic_slice_in_dim(taper[0], mem * n_half, n_half, axis=1).astype(BF)
    taper_own = lax.all_gather(taper_own, "lat", axis=0, tiled=True)
    taper_other = lax.ppermute(taper_own, "mem", SWAP)

    tables = bases(cols, blocks, padded, lat_total)
    dims = (cols, blocks, bands, padded, coefs, lat_total)
    summed = None
    for i, field in enumerate(chunks):
        summed = member(
            place, field, (innov_own, innov_other), (taper_own, taper_other), tables, summed,
            i == len(chunks) - 1, dims,
        )
    own, other = summed
    arrived = lax.ppermute(other, "mem", SWAP)
    merged = (own + arrived.astype(F32)).astype(BF)
    pieces = over_all(merged).reshape(bands, levels, half, lat_rows)
    total = jnp.sum(pieces.astype(F32), axis=0) / (ensemble - 1)
    both = lax.all_gather(total, "mem", axis=0)
    return jnp.concatenate([both[0], both[1][:, : cols - half, :]], axis=1)


def solution(mesh):
    in_specs = (
        P("mem", None, "lon", "lat"),
        P("lon", "lat", None),
        P("lat", "lon"),
        P("lat", "lon"),
        P("lat", "lon"),
        P("lat", "lon"),
    )
    out_specs = P(None, "lon", "lat")
    return jax.shard_map(local, mesh=mesh, in_specs=in_specs, out_specs=out_specs, check_vma=False)
```

profile of v0, /device:TPU:1, one launch (start us, length us, event | category | flops | bytes accessed | tf_op | source)
XLA Modules:
  0.0 233.9 jit_solution(9997123541347237032)
XLA Ops:
  0.0 0.0 copy-start
  0.0 0.1 pad_add_fusion.refs_0_
  0.1 0.0 copy-start.13
  0.1 0.8 copy-done.13
  0.9 0.0 copy-start.14
  0.9 0.8 copy-done.14
  1.7 0.0 copy-start.15
  1.7 0.8 copy-done.15
  2.4 0.0 copy-start.16
  2.4 0.8 copy-done.16
  3.2 6.6 %spread.1 = bf16[4,16,48,128]{3,2,1,0:T(8,128)(2,1)} custom-call(s32[3]{0:T(128)S(1)} %pad_add_fusion.refs_0_, s32[64,128]{1,0:T(8,128)S(1)} %copy-done.13, s32[64,128]{1,0:T(8,128)S(1)} %copy-done.14, s32[64,128]{1,0:T(8,128)S(1)} %copy-done.15, f32[64,128]{1,0:T(8,128)S(1)} %copy-done.16), custom_call_target="tpu_custom_call" | custom-call | tf_op jit(solution)/shard_map/spread/pallas_call | solution.py:72
  9.7 11.9 %all-to-all-start.1 = ((bf16[64,48,128]{2,1,0:T(8,128)(2,1)}), bf16[64,48,128]{2,1,0:T(8,128)(2,1)S(1)}, u32[]{:S(2)}, u32[]{:S(2)}) async-start(bf16[64,48,128]{2,1,0:T(8,128)(2,1)} %bitcast.4), calls=%async_computation.1 | async-start | bytes 1572864 | tf_op jit(solution)/shard_map/all_to_all | solution.py:29
  21.7 4.6 %fusion = (bf16[4,16,90,128]{3,1,2,0:T(8,128)(2,1)S(1)}, bf16[4,16,90,128]{3,1,2,0:T(8,128)(2,1)}, bf16[4,16,90,128]{3,1,2,0:T(8,128)(2,1)}) fusion(bf16[12,16,90,128]{3,1,2,0:T(8,128)(2,1)} %param.6), kind=kLoop, calls=%fused_computation.6 | loop fusion | bytes 8847360 | tf_op jit(solution)/shard_map/slice | solution.py:276
  26.3 1.6 copy.16
  27.9 8.7 %all-to-all-done.1.refs_2_ = bf16[64,48,128]{2,1,0:T(8,128)(2,1)S(1)} async-done(((bf16[64,48,128]{2,1,0:T(8,128)(2,1)}), bf16[64,48,128]{2,1,0:T(8,128)(2,1)S(1)}, u32[]{:S(2)}, u32[]{:S(2)}) %all-to-all-start.1) | async-done | bytes 786464 | tf_op jit(solution)/shard_map/all_to_all | solution.py:29
  36.5 4.7 %all-to-all-start.3 = ((bf16[64,90,128]{2,1,0:T(8,128)(2,1)}), bf16[64,90,128]{2,1,0:T(8,128)(2,1)S(1)}, u32[]{:S(2)}, u32[]{:S(2)}) async-start(bf16[64,90,128]{2,1,0:T(8,128)(2,1)} %bitcast.16), calls=%async_computation.3 | async-start | bytes 3145728 | tf_op jit(solution)/shard_map/all_to_all | solution.py:29
  41.2 3.0 %copy.15 = bf16[4,16,90,128]{3,2,1,0:T(8,128)(2,1)} copy(bf16[4,16,90,128]{3,1,2,0:T(8,128)(2,1)} %get-tuple-element.19) | data formatting | bytes 2949120 | tf_op jit(solution)/shard_map/slice | solution.py:276
  44.2 19.6 %all-to-all-done.3.refs_1_ = bf16[64,90,128]{2,1,0:T(8,128)(2,1)S(1)} async-done(((bf16[64,90,128]{2,1,0:T(8,128)(2,1)}), bf16[64,90,128]{2,1,0:T(8,128)(2,1)S(1)}, u32[]{:S(2)}, u32[]{:S(2)}) %all-to-all-start.3) | async-done | bytes 1474592 | tf_op jit(solution)/shard_map/all_to_all | solution.py:29
  63.8 0.0 copy-start.7
  63.8 1.1 copy-done.7
  64.9 5.0 %all-to-all-start.2 = ((bf16[64,90,128]{2,1,0:T(8,128)(2,1)}), bf16[64,90,128]{2,1,0:T(8,128)(2,1)S(1)}, u32[]{:S(2)}, u32[]{:S(2)}) async-start(bf16[64,90,128]{2,1,0:T(8,128)(2,1)} %bitcast.15), calls=%async_computation.2 | async-start | bytes 3145728 | tf_op jit(solution)/shard_map/all_to_all | solution.py:29
  69.9 3.0 %copy.14 = bf16[4,16,90,128]{3,2,1,0:T(8,128)(2,1)} copy(bf16[4,16,90,128]{3,1,2,0:T(8,128)(2,1)} %get-tuple-element.18) | data formatting | bytes 2949120 | tf_op jit(solution)/shard_map/slice | solution.py:276
  72.9 19.0 %all-to-all-done.2.refs_1_ = bf16[64,90,128]{2,1,0:T(8,128)(2,1)S(1)} async-done(((bf16[64,90,128]{2,1,0:T(8,128)(2,1)}), bf16[64,90,128]{2,1,0:T(8,128)(2,1)S(1)}, u32[]{:S(2)}, u32[]{:S(2)}) %all-to-all-start.2) | async-done | bytes 1474592 | tf_op jit(solution)/shard_map/all_to_all | solution.py:29
  91.9 0.0 copy-start.5
  91.9 1.2 copy-done.5
  93.1 5.5 %all-to-all-start = ((bf16[64,90,128]{2,1,0:T(8,128)(2,1)}), bf16[64,90,128]{2,1,0:T(8,128)(2,1)}, u32[]{:S(2)}, u32[]{:S(2)}) async-start(bf16[64,90,128]{2,1,0:T(8,128)(2,1)} %bitcast.14), calls=%async_computation | async-start | bytes 3145728 | tf_op jit(solution)/shard_map/all_to_all | solution.py:29
  98.6 0.0 copy-done
  98.6 3.6 %collective-permute-start = (bf16[64,48,128]{2,1,0:T(8,128)(2,1)S(1)}, bf16[64,48,128]{2,1,0:T(8,128)(2,1)S(1)}, u32[]{:S(2)}, u32[]{:S(2)}) collective-permute-start(bf16[64,48,128]{2,1,0:T(8,128)(2,1)S(1)} %all-to-all-done.1.refs_2_), channel_id=1, source_target_pairs={{0,1},{1,0},{2,3},{3,2},{4,5},{5,4},{6,7},{7,6},{8,9},{9,8},{10,11... | collective-permute-start | bytes 2359304 | tf_op jit(solution)/shard_map/ppermute | solution.py:282
  102.2 24.3 %all-gather = bf16[1,1440,256]{2,1,0:T(8,128)(2,1)S(1)} all-gather(bf16[1,360,256]{2,1,0:T(8,128)(2,1)S(1)} %dynamic-slice_convert_fusion), channel_id=2, replica_groups=mesh['lat'=4,'lon'=16,'mem'=2] {'lat'}, dimensions={1}, use_global_device_ids=true | all-gather | bytes 921600 | tf_op jit(solution)/shard_map/all_gather | solution.py:286
  126.5 2.9 %collective-permute-start.1 = (bf16[1440,256]{1,0:T(8,128)(2,1)S(1)}, bf16[1440,256]{1,0:T(8,128)(2,1)S(1)}, u32[]{:S(2)}, u32[]{:S(2)}) collective-permute-start(bf16[1440,256]{1,0:T(8,128)(2,1)S(1)} %bitcast.10), channel_id=1, source_target_pairs={{0,1},{1,0},{2,3},{3,2},{4,5},{5,4},{6,7},{7,6},{8,9},{9,8},{10,11... | collective-permute-start | bytes 2211848 | tf_op jit(solution)/shard_map/ppermute | solution.py:287
  129.4 19.8 %bases.1 = (bf16[1536,1536]{1,0:T(8,128)(2,1)S(1)}, bf16[1536,1536]{1,0:T(8,128)(2,1)S(1)}, bf16[512,512]{1,0:T(8,128)(2,1)S(1)}, bf16[512,512]{1,0:T(8,128)(2,1)S(1)}) custom-call(), custom_call_target="tpu_custom_call" | custom-call | tf_op jit(solution)/shard_map/bases/pallas_call | solution.py:147
  149.3 0.0 copy-start.1
  149.3 2.1 copy-done.1
  151.4 0.0 copy-start.2
  151.4 2.2 copy-done.2
  153.6 0.0 copy-start.9
  153.6 0.0 copy-start.11
  153.6 0.0 collective-permute-done.1.refs_5_
  153.6 0.0 copy-start.3
  153.6 0.0 collective-permute-done.refs_3_
  153.6 0.0 copy-start.8
  153.6 2.0 copy-done.8
  155.7 0.0 copy-start.6
  155.7 13.8 %member.3.refs_10_ = f32[64,96,128]{2,1,0:T(8,128)} custom-call(s32[3]{0:T(128)S(1)} %pad_add_fusion.refs_0_, bf16[64,90,128]{2,1,0:T(8,128)(2,1)S(1)} %copy-done.8, bf16[64,48,128]{2,1,0:T(8,128)(2,1)S(1)} %all-to-all-done.1.refs_2_, bf16[64,48,128]{2,1,0:T(8,128)(2,1)S(1)} %collective-permute-done.refs_3_, bf16[1440,256]{1,0:T(8,128)(2,1)S(1)} %bitcast.11, ...), custom_call_target="tpu_custom_call" | custom-call | tf_op jit(solution)/shard_map/member/pallas_call | solution.py:250
  169.4 0.0 copy-done.9
  169.4 0.0 copy-done.11
  169.4 0.0 copy-done.3
  169.4 0.0 copy-done.6
  169.5 14.6 %member.4.refs_10_ = f32[64,96,128]{2,1,0:T(8,128)} custom-call(s32[3]{0:T(128)S(1)} %pad_add_fusion.refs_0_, bf16[64,90,128]{2,1,0:T(8,128)(2,1)S(1)} %copy-done.6, bf16[64,48,128]{2,1,0:T(8,128)(2,1)S(1)} %all-to-all-done.1.refs_2_, bf16[64,48,128]{2,1,0:T(8,128)(2,1)S(1)} %collective-permute-done.refs_3_, bf16[1440,256]{1,0:T(8,128)(2,1)S(1)} %bitcast.12, ...), custom_call_target="tpu_custom_call" | custom-call | tf_op jit(solution)/shard_map/member/pallas_call | solution.py:250
  184.0 0.0 all-to-all-done.refs_1_
  184.0 1.1 copy-done.4
  185.2 0.0 copy-start.10
  185.2 1.0 copy-done.10
  186.2 0.0 copy-start.12
  186.2 1.0 copy-done.12
  187.2 14.7 %member.5 = (f32[64,48,128]{2,1,0:T(8,128)}, bf16[64,48,128]{2,1,0:T(8,128)(2,1)S(1)}) custom-call(s32[3]{0:T(128)S(1)} %pad_add_fusion.refs_0_, bf16[64,90,128]{2,1,0:T(8,128)(2,1)} %all-to-all-done.refs_1_, bf16[64,48,128]{2,1,0:T(8,128)(2,1)S(1)} %all-to-all-done.1.refs_2_, bf16[64,48,128]{2,1,0:T(8,128)(2,1)S(1)} %collective-permute-done.refs_3_, ...), custom_call_target="tpu_custom_call" | custom-call | tf_op jit(solution)/shard_map/member/pallas_call | solution.py:250
  202.0 0.0 collective-permute-start.2
  202.0 2.3 collective-permute-done.2
  204.2 1.6 add_convert_fusion
  205.8 22.9 %all_to_all.25 = bf16[64,48,128]{2,1,0:T(8,128)(2,1)S(1)} all-to-all(bf16[64,48,128]{2,1,0:T(8,128)(2,1)S(1)} %add_convert_fusion), channel_id=1, replica_groups=mesh['lat'=4,'lon'=16,'mem'=2] {'lat','lon'}, dimensions={0} | all-to-all | bytes 1572864 | tf_op jit(solution)/shard_map/all_to_all | solution.py:29
  228.7 0.1 convert_reduce_fusion
  228.9 3.6 %all-gather.1 = f32[32,48,128]{2,1,0:T(8,128)S(1)} all-gather(f32[16,48,128]{2,1,0:T(8,128)S(1)} %broadcast_multiply_fusion), channel_id=3, replica_groups=mesh['lat'=4,'lon'=16,'mem'=2] {'mem'}, dimensions={0}, use_global_device_ids=true | all-gather | bytes 1179648 | tf_op jit(solution)/shard_map/all_gather | solution.py:302
  232.5 0.1 pad_maximum_fusion
  232.6 1.3 copy.17
  (5 shorter events, 0.1 us)
Async XLA Ops:
  0.0 98.6 %copy-start = (f32[1,360,512]{2,1,0:T(8,128)S(1)}, f32[1,360,512]{2,1,0:T(8,128)}, u32[]{:S(2)}) copy-start(f32[1,360,512]{2,1,0:T(8,128)} %param.7) | copy-start | bytes 2211844
  0.1 0.8 copy-start.13
  0.9 0.8 copy-start.14
  1.7 0.8 copy-start.15
  2.4 0.8 copy-start.16
  9.7 26.8 %all-to-all-start.1 = ((bf16[64,48,128]{2,1,0:T(8,128)(2,1)}), bf16[64,48,128]{2,1,0:T(8,128)(2,1)S(1)}, u32[]{:S(2)}, u32[]{:S(2)}) async-start(bf16[64,48,128]{2,1,0:T(8,128)(2,1)} %bitcast.4), calls=%async_computation.1 | async-start | bytes 1572864 | tf_op jit(solution)/shard_map/all_to_all | solution.py:29
  36.5 27.2 %all-to-all-start.3 = ((bf16[64,90,128]{2,1,0:T(8,128)(2,1)}), bf16[64,90,128]{2,1,0:T(8,128)(2,1)S(1)}, u32[]{:S(2)}, u32[]{:S(2)}) async-start(bf16[64,90,128]{2,1,0:T(8,128)(2,1)} %bitcast.16), calls=%async_computation.3 | async-start | bytes 3145728 | tf_op jit(solution)/shard_map/all_to_all | solution.py:29
  63.8 1.1 copy-start.7
  64.9 27.0 %all-to-all-start.2 = ((bf16[64,90,128]{2,1,0:T(8,128)(2,1)}), bf16[64,90,128]{2,1,0:T(8,128)(2,1)S(1)}, u32[]{:S(2)}, u32[]{:S(2)}) async-start(bf16[64,90,128]{2,1,0:T(8,128)(2,1)} %bitcast.15), calls=%async_computation.2 | async-start | bytes 3145728 | tf_op jit(solution)/shard_map/all_to_all | solution.py:29
  91.9 1.2 copy-start.5
  93.1 91.0 %all-to-all-start = ((bf16[64,90,128]{2,1,0:T(8,128)(2,1)}), bf16[64,90,128]{2,1,0:T(8,128)(2,1)}, u32[]{:S(2)}, u32[]{:S(2)}) async-start(bf16[64,90,128]{2,1,0:T(8,128)(2,1)} %bitcast.14), calls=%async_computation | async-start | bytes 3145728 | tf_op jit(solution)/shard_map/all_to_all | solution.py:29
  98.6 55.0 %collective-permute-start = (bf16[64,48,128]{2,1,0:T(8,128)(2,1)S(1)}, bf16[64,48,128]{2,1,0:T(8,128)(2,1)S(1)}, u32[]{:S(2)}, u32[]{:S(2)}) collective-permute-start(bf16[64,48,128]{2,1,0:T(8,128)(2,1)S(1)} %all-to-all-done.1.refs_2_), channel_id=1, source_target_pairs={{0,1},{1,0},{2,3},{3,2},{4,5},{5,4},{6,7},{7,6},{8,9},{9,8},{10,11... | collective-permute-start | bytes 2359304 | tf_op jit(solution)/shard_map/ppermute | solution.py:282
  126.5 27.1 %collective-permute-start.1 = (bf16[1440,256]{1,0:T(8,128)(2,1)S(1)}, bf16[1440,256]{1,0:T(8,128)(2,1)S(1)}, u32[]{:S(2)}, u32[]{:S(2)}) collective-permute-start(bf16[1440,256]{1,0:T(8,128)(2,1)S(1)} %bitcast.10), channel_id=1, source_target_pairs={{0,1},{1,0},{2,3},{3,2},{4,5},{5,4},{6,7},{7,6},{8,9},{9,8},{10,11... | collective-permute-start | bytes 2211848 | tf_op jit(solution)/shard_map/ppermute | solution.py:287
  149.3 2.2 copy-start.1
  151.4 2.2 copy-start.2
  153.6 15.8 %copy-start.9 = (bf16[512,512]{1,0:T(8,128)(2,1)}, bf16[512,512]{1,0:T(8,128)(2,1)S(1)}, u32[]{:S(2)}) copy-start(bf16[512,512]{1,0:T(8,128)(2,1)S(1)} %get-tuple-element.13.refs_8_) | copy-start | bytes 1572868
  153.6 15.8 %copy-start.11 = (bf16[512,512]{1,0:T(8,128)(2,1)}, bf16[512,512]{1,0:T(8,128)(2,1)S(1)}, u32[]{:S(2)}) copy-start(bf16[512,512]{1,0:T(8,128)(2,1)S(1)} %get-tuple-element.14.refs_9_) | copy-start | bytes 1572868
  153.6 15.8 %copy-start.3 = (bf16[1440,256]{1,0:T(8,128)(2,1)}, bf16[1440,256]{1,0:T(8,128)(2,1)S(1)}, u32[]{:S(2)}) copy-start(bf16[1440,256]{1,0:T(8,128)(2,1)S(1)} %collective-permute-done.1.refs_5_) | copy-start | bytes 2211844
  153.6 2.0 copy-start.8
  155.7 13.8 %copy-start.6 = (bf16[64,90,128]{2,1,0:T(8,128)(2,1)S(1)}, bf16[64,90,128]{2,1,0:T(8,128)(2,1)}, u32[]{:S(2)}) copy-start(bf16[64,90,128]{2,1,0:T(8,128)(2,1)} %copy-done.5) | copy-start | bytes 4423684
  184.0 1.1 copy-start.4
  185.2 1.0 copy-start.10
  186.2 1.0 copy-start.12
  202.0 2.3 collective-permute-start.2
where the time goes:
time: 235 us; the launch traced here: 234 us
  Pallas kernels  69.4 us (30%)
  blocking collectives  50.8 us (22%)
  waiting for transfers between devices  49.5 us (21%)
  starting transfers between devices  33.6 us (14%)
  local copies, waits for them, and re-layouts  28.5 us (12%)
    all_to_all x4, waiting for transfers between devices, over_all(): return lax.all_to_all(x, LL, split_axis=0, concat_axis=0, tiled=True)  47.3 us
    pallas_call x3, Pallas kernels, member(): pl.pallas_call(lambda *refs: member_kernel(*refs, first=first, final=fina...  43.1 us
    all_to_all x4, starting transfers between devices, over_all(): return lax.all_to_all(x, LL, split_axis=0, concat_axis=0, tiled=True)  27.1 us
    all_gather x1, blocking collectives, local(): taper_own = lax.all_gather(taper_own, 'lat', axis=0, tiled=True)  24.3 us
    all_to_all x1, blocking collectives, over_all(): return lax.all_to_all(x, LL, split_axis=0, concat_axis=0, tiled=True)  22.9 us
    pallas_call x1, Pallas kernels, bases(): pl.pallas_call(lambda *refs: basis_kernel(*refs, cols=cols, blocks=blocks...  19.8 us
    unnamed x34, local copies, waits for them, and re-layouts  15 us
    slice x4, local copies, waits for them, and re-layouts, local(): anomalies[i:i + bands].reshape(bands * levels, cols, lat_rows)  12.1 us
  transfers between devices with their start and end apart: 7, of which 4 were waited for; matrix products, arithmetic and copies ran while one was open for 5% of the time, Pallas kernels for 21%

commit v1 on v0

v1 whole, which is shorter than its diff:
```python
import math

import jax
import jax.numpy as jnp
from jax import lax
from jax.experimental import pallas as pl
from jax.experimental.pallas import tpu as pltpu
from jax.sharding import PartitionSpec as P


BF = jnp.bfloat16
F32 = jnp.float32
LL = ("lat", "lon")
SWAP = [(0, 1), (1, 0)]
RING = 4


def vspec():
    return pl.BlockSpec(memory_space=pltpu.VMEM)


def sspec():
    return pl.BlockSpec(memory_space=pltpu.SMEM)


def params(mib, **more):
    return pltpu.CompilerParams(vmem_limit_bytes=mib * 1024 * 1024, **more)


def cost(flops):
    return pl.CostEstimate(flops=int(flops), bytes_accessed=1 << 20, transcendentals=0)


def over_all(x):
    return lax.all_to_all(x, LL, split_axis=0, concat_axis=0, tiled=True)


def shift_lat(x, s):
    return lax.ppermute(x, "lat", [(i, (i + s) % RING) for i in range(RING)])


def shift_z(x, s):
    return lax.ppermute(
        x, "lon", [(z * RING + i, (z + s) % RING * RING + i) for z in range(RING) for i in range(RING)]
    )


def shift_x(x, s):
    return lax.ppermute(
        x, "lon", [(z * RING + i, z * RING + (i + s) % RING) for z in range(RING) for i in range(RING)]
    )


def swap(x):
    return lax.ppermute(x, "mem", SWAP)


def relayout_kernel(in_ref, out_ref, *, split, cols, levels, padded):
    size = 16 * levels
    to = lax.broadcasted_iota(jnp.int32, (size, size), 0)
    frm = lax.broadcasted_iota(jnp.int32, (size, size), 1)
    turn = jnp.where(frm == (to & 15) * levels + (to >> 4), 1.0, 0.0).astype(BF)
    for start in range(0, padded, 16):
        have = min(16, cols - start)
        parts = []
        for p in range(2):
            block = in_ref[(p, 0) if split else (0, p)][start : start + have]
            parts.append(block.reshape(have * levels, 128))
        both = jnp.concatenate(parts, axis=1)
        if have < 16:
            both = jnp.concatenate([both, jnp.zeros(((16 - have) * levels, 256), BF)], axis=0)
        turned = jnp.dot(turn, both, preferred_element_type=F32).astype(BF)
        for l in range(levels):
            for p in range(2):
                piece = turned[16 * l : 16 * l + 16, 128 * p : 128 * p + 128]
                if split:
                    out_ref[l, p, start : start + 16, :] = piece
                else:
                    out_ref[p * levels + l, 0, start : start + 16, :] = piece


def relayout(fields, pair, padded):
    rounds, bands, cols, levels, lanes = fields.shape
    kernel = lambda i, o: relayout_kernel(i, o, split=pair, cols=cols, levels=levels, padded=padded)
    if pair:
        return pl.pallas_call(
            kernel,
            grid=(bands,),
            in_specs=[pl.BlockSpec((2, 1, cols, levels, lanes), lambda g: (0, g, 0, 0, 0))],
            out_specs=pl.BlockSpec((levels, 2, padded, lanes), lambda g: (g, 0, 0, 0)),
            out_shape=jax.ShapeDtypeStruct((bands * levels, 2, padded, lanes), BF),
            compiler_params=params(12),
            name="relayout_pair",
        )(fields)
    return pl.pallas_call(
        kernel,
        grid=(bands // 2,),
        in_specs=[pl.BlockSpec((1, 2, cols, levels, lanes), lambda g: (rounds - 1, g, 0, 0, 0))],
        out_specs=pl.BlockSpec((2 * levels, 1, padded, lanes), lambda g: (g, 0, 0, 0)),
        out_shape=jax.ShapeDtypeStruct((bands * levels, 1, padded, lanes), BF),
        compiler_params=params(12),
        name="relayout_last",
    )(fields)


def spread_kernel(place, row_ref, col_ref, level_ref, value_ref, out_ref, acc, *, half, levels, cols):
    mem, lat, z, x = place[0], place[1], place[2], place[3]
    slots = levels * half
    col_start = (z * RING + x) * cols + mem * half
    acc[...] = jnp.zeros_like(acc)
    slot_ids = lax.broadcasted_iota(jnp.int32, (slots, 128), 0)
    row_ids = lax.broadcasted_iota(jnp.int32, (128, 128), 0)

    def add_group(g, carry):
        rows = pl.ds(pl.multiple_of(g * 8, 8), 8)
        within = col_ref[rows, :] - col_start
        inside = (within >= 0) & (within < half)
        keys = jnp.where(inside, level_ref[rows, :] * half + within, -1)
        lat_row = row_ref[rows, :] - lat * 128
        value = value_ref[rows, :]
        high = value.astype(BF).astype(F32)
        middle = value - high
        left = []
        right = []
        for r in range(8):
            hit = slot_ids == keys[r : r + 1, :]
            left.append(jnp.where(hit, 1.0, 0.0).astype(BF))
            row_hit = row_ids == lat_row[r : r + 1, :]
            top = jnp.where(row_hit, high[r : r + 1, :], 0.0)
            low = jnp.where(row_hit, middle[r : r + 1, :], 0.0)
            right.append(jnp.concatenate([top, low], axis=0).astype(BF))
        acc[...] += lax.dot_general(
            jnp.concatenate(left, axis=1),
            jnp.concatenate(right, axis=1),
            (((1,), (1,)), ((), ())),
            preferred_element_type=F32,
        )
        return carry

    lax.fori_loop(0, row_ref.shape[0] // 8, add_group, 0)
    for s in range(RING):
        for t in range(RING):
            level = lax.rem(z + s, RING) * RING + lax.rem(x + t, RING)
            rows = pl.ds(pl.multiple_of(level * half, 8), half)
            out_ref[s, t] = (acc[rows, :128] + acc[rows, 128:]).astype(BF)


def spread(place, obs_row, obs_col, obs_level, obs_value, half, levels, cols):
    return pl.pallas_call(
        lambda *refs: spread_kernel(*refs, half=half, levels=levels, cols=cols),
        out_shape=jax.ShapeDtypeStruct((RING, RING, half, 128), BF),
        in_specs=[sspec()] + [vspec()] * 4,
        out_specs=vspec(),
        scratch_shapes=[pltpu.VMEM((levels * half, 256), F32)],
        compiler_params=params(14),
        cost_estimate=cost(6e9),
        name="spread",
    )(place, obs_row, obs_col, obs_level, obs_value)


def turn_cos(turns):
    near = 0.25 - jnp.abs(turns - jnp.floor(turns + 0.5))
    square = near * near
    value = jnp.full_like(square, -15.094642576822990)
    for factor in (42.058693944897653, -76.705859753061386, 81.605249276075055, -41.341702240399755):
        value = value * square + factor
    return near * (value * square + 6.283185307179586)


def basis_kernel(lon_ref, lon_t_ref, lat_ref, lat_t_ref, *, cols, blocks, padded):
    total = cols * blocks
    half = total // 2
    tiles = lon_ref.shape[1] // 128
    lanes = lax.broadcasted_iota(jnp.int32, (padded, 128), 1)

    def turns_of(product):
        whole = (product.astype(F32) * (1.0 / total)).astype(jnp.int32)
        return (product - whole * total).astype(F32) * (1.0 / total)

    def lon_rows(j, carry):
        within = lax.broadcasted_iota(jnp.int32, (padded, 128), 0)
        x = within + cols * j
        fine = turns_of(x * lanes)
        coarse = turns_of(x * (lanes * 128))
        fine_cos = turn_cos(fine)
        fine_sin = turn_cos(fine - 0.25)
        scale = jnp.where(within < cols, math.sqrt(2.0 / total), 0.0)
        coarse_cos = turn_cos(coarse) * scale
        coarse_sin = turn_cos(coarse - 0.25) * scale
        sign = jnp.where((x & 1) == 0, 1.0, -1.0)
        rows = pl.ds(pl.multiple_of(j * padded, padded), padded)
        for t in range(tiles):
            c = lanes + 128 * t
            cos_t = coarse_cos[:, t : t + 1]
            sin_t = coarse_sin[:, t : t + 1]
            parts = []
            if 128 * t <= half:
                parts.append(fine_cos * cos_t - fine_sin * sin_t)
            if 128 * t + 127 > half:
                parts.append((fine_sin * cos_t + fine_cos * sin_t) * sign)
            value = parts[0] if len(parts) == 1 else jnp.where(c <= half, parts[0], parts[1])
            if t == 0 or 128 * t <= half < 128 * t + 128:
                value = jnp.where((c == 0) | (c == half), value * math.sqrt(0.5), value)
            if 128 * t + 127 >= total:
                value = jnp.where(c < total, value, 0.0)
            lon_ref[rows, 128 * t : 128 * t + 128] = value.astype(BF)
        return carry

    lax.fori_loop(0, blocks, lon_rows, 0)
    for t in range(tiles):
        strip = lon_ref[:, 128 * t : 128 * t + 128].astype(F32)
        lon_t_ref[128 * t : 128 * t + 128, :] = strip.T.astype(BF)

    length = lat_ref.shape[0]
    step = 64

    def lat_rows(i, carry):
        shape = (step, length)
        down = lax.broadcasted_iota(jnp.int32, shape, 0) + step * i
        across = lax.broadcasted_iota(jnp.int32, shape, 1)
        rows = pl.ds(pl.multiple_of(i * step, step), step)
        for grid, mode, ref in ((down, across, lat_ref), (across, down, lat_t_ref)):
            phase = (mode * (2 * grid + 1)) & (4 * length - 1)
            scale = jnp.where(mode == 0, 1.0 / math.sqrt(length), math.sqrt(2.0 / length))
            ref[rows, :] = (turn_cos(phase.astype(F32) * (0.25 / length)) * scale).astype(BF)
        return carry

    lax.fori_loop(0, length // step, lat_rows, 0)


def bases(cols, blocks, padded, lat_total):
    wide = padded * blocks
    return pl.pallas_call(
        lambda *refs: basis_kernel(*refs, cols=cols, blocks=blocks, padded=padded),
        out_shape=(
            jax.ShapeDtypeStruct((wide, wide), BF),
            jax.ShapeDtypeStruct((wide, wide), BF),
            jax.ShapeDtypeStruct((lat_total, lat_total), BF),
            jax.ShapeDtypeStruct((lat_total, lat_total), BF),
        ),
        out_specs=(vspec(),) * 4,
        compiler_params=params(20),
        cost_estimate=cost(12e9),
        name="bases",
    )()


def arrange_kernel(place, own, other, innov, taper, *, half, blocks, rows_each):
    mem, lat, z, x = place[0], place[1], place[2], place[3]
    packed = blocks * half
    for ref, side in ((own, mem), (other, 1 - mem)):
        rows = pl.ds(pl.multiple_of(side * half, 16), half)
        for u in range(RING):
            band = lax.rem(lat + RING - u, RING)
            for t in range(RING):
                for s in range(RING):
                    j = lax.rem(z + RING - s, RING) * RING + lax.rem(x + RING - t, RING)
                    start = (t * RING + s) * half
                    innov[band * blocks + j, rows, :] = ref[u, start : start + half, :]
            into = pl.ds(pl.multiple_of(band * rows_each, 8), rows_each)
            for q in range(2):
                start = packed + q * rows_each
                taper[2 * side + q, into, :] = ref[u, start : start + rows_each, :]


def arrange(place, own, other, half, blocks, padded, rows_each):
    return pl.pallas_call(
        lambda *refs: arrange_kernel(*refs, half=half, blocks=blocks, rows_each=rows_each),
        out_shape=(
            jax.ShapeDtypeStruct((RING * blocks, padded, 128), BF),
            jax.ShapeDtypeStruct((4, RING * rows_each, 128), BF),
        ),
        in_specs=[sspec(), vspec(), vspec()],
        out_specs=(vspec(), vspec()),
        compiler_params=params(12),
        cost_estimate=cost(1e9),
        name="arrange",
    )(place, own, other)


def member_kernel(*refs, first, final, blocks, bands, padded, coefs):
    place, field, innov_hbm, taper_hbm, lon_hbm, lon_t_hbm, lat_hbm, lat_t_hbm = refs[:8]
    rest = list(refs[8:])
    so_far_hbm = None if first else rest.pop(0)
    if final:
        own_out, other_out, acc = rest[0], rest[1], rest.pop()
        rest = rest[2:]
    else:
        acc = rest.pop(0)
    weighted, inverse, innov, taper, lon_ref, lon_t_ref, lat_ref, lat_t_ref, sems = rest
    wide = padded * blocks
    step = coefs // 3
    group = 4
    tall = group * padded
    count = iter(range(16))

    def fetch(source, target):
        copy = pltpu.make_async_copy(source, target, sems.at[next(count)])
        copy.start()
        return copy

    innov_copy = fetch(innov_hbm, innov)
    lon_t_copies = [fetch(lon_t_hbm.at[pl.ds(0, step)], lon_t_ref.at[pl.ds(0, step)])]
    lat_copies = [fetch(lat_hbm, lat_ref), fetch(taper_hbm, taper), fetch(lat_t_hbm, lat_t_ref)]
    lon_t_copies += [
        fetch(lon_t_hbm.at[pl.ds(r * step, step)], lon_t_ref.at[pl.ds(r * step, step)]) for r in (1, 2)
    ]
    lon_copies = [
        fetch(lon_hbm.at[pl.ds(b * tall, tall)], lon_ref.at[pl.ds(b * tall, tall)]) for b in range(blocks // group)
    ]
    if not first:
        lon_copies.append(fetch(so_far_hbm, acc))
    inverse[coefs:, :] = jnp.zeros((wide - coefs, inverse.shape[1]), BF)
    innov_copy.wait()

    def weigh(i):
        def body(j, carry):
            rows = pl.ds(pl.multiple_of(j * padded, padded), padded)
            for a in range(bands):
                spot = a * blocks + j
                weighted[rows, 128 * a : 128 * a + 128] = field[spot, i] * innov[spot]
            return carry

        lax.fori_loop(0, blocks, body, 0)

    def spectral(r, carry):
        rows = pl.ds(pl.multiple_of(r * step, 16), step)
        zonal = jnp.dot(lon_t_ref[rows, :], weighted[...], preferred_element_type=F32).astype(BF)
        spectrum = jnp.dot(zonal, lat_ref[...], preferred_element_type=F32)
        weights = jnp.concatenate([taper[q, rows, :] for q in range(4)], axis=1).astype(F32)
        tapered = (spectrum * weights).astype(BF)
        inverse[rows, :] = jnp.dot(tapered, lat_t_ref[...], preferred_element_type=F32).astype(BF)
        return carry

    def gridded(i):
        def body(b, carry):
            rows = pl.ds(pl.multiple_of(b * tall, tall), tall)
            localized = jnp.dot(lon_ref[rows, :], inverse[...], preferred_element_type=F32)
            for g in range(group):
                for a in range(bands):
                    spot = a * blocks + b * group + g
                    piece = localized[g * padded : (g + 1) * padded, 128 * a : 128 * a + 128]
                    piece = piece * field[spot, i].astype(F32)
                    acc[spot] = piece if first and i == 0 else piece + acc[spot]
            return carry

        lax.fori_loop(0, blocks // group, body, 0)

    for i in range(field.shape[1]):
        weigh(i)
        if i == 0:
            for copy in [lon_t_copies[0], *lat_copies]:
                copy.wait()
            for copy in lon_t_copies[1:]:
                copy.wait()
        lax.fori_loop(0, coefs // step, spectral, 0)
        if i == 0:
            for copy in lon_copies:
                copy.wait()
        gridded(i)
    if final:
        half = padded // 2
        mem = place[0]
        own_out[...] = acc[:, pl.ds(pl.multiple_of(mem * half, half), half), :]
        other_out[...] = acc[:, pl.ds(pl.multiple_of((1 - mem) * half, half), half), :].astype(BF)


def member(place, field, innov, taper, tables, so_far, final, dims):
    _, blocks, bands, padded, coefs, lat_total = dims
    spots = bands * blocks
    half = padded // 2
    wide = padded * blocks
    first = so_far is None
    far = [innov, taper, *tables] + ([] if first else [so_far])
    scratch = [pltpu.VMEM((wide, lat_total), BF), pltpu.VMEM((wide, lat_total), BF)]
    scratch += [pltpu.VMEM(array.shape, array.dtype) for array in (innov, taper, *tables)]
    scratch.append(pltpu.SemaphoreType.DMA((16,)))
    if final:
        out_shape = (
            jax.ShapeDtypeStruct((spots, half, 128), F32),
            jax.ShapeDtypeStruct((spots, half, 128), BF),
        )
        out_specs = (vspec(), vspec())
        scratch.append(pltpu.VMEM((spots, padded, 128), F32))
    else:
        out_shape = jax.ShapeDtypeStruct((spots, padded, 128), F32)
        out_specs = vspec()
    return pl.pallas_call(
        lambda *refs: member_kernel(
            *refs, first=first, final=final, blocks=blocks, bands=bands, padded=padded, coefs=coefs
        ),
        out_shape=out_shape,
        in_specs=[sspec(), vspec()] + [pl.BlockSpec(memory_space=pltpu.HBM)] * len(far),
        out_specs=out_specs,
        scratch_shapes=scratch,
        compiler_params=params(44),
        cost_estimate=cost(field.shape[1] * 6e9),
        name="member_last" if final else "member_pair",
    )(place, field, *far)


def finish_kernel(place, own, other, out, *, levels, cols, half, scale):
    mem = place[0]
    bands = own.shape[0] // levels
    for side in range(2):
        rows = min(half, cols - side * half)
        for l in range(levels):
            mine = sum(own[a * levels + l].astype(F32) for a in range(bands))
            theirs = sum(other[a * levels + l].astype(F32) for a in range(bands))
            total = jnp.where(mem == side, mine, theirs) * scale
            out[side * half : side * half + rows, l, :] = total[:rows]


def finish(place, own, other, levels, cols, half, scale):
    return pl.pallas_call(
        lambda *refs: finish_kernel(*refs, levels=levels, cols=cols, half=half, scale=scale),
        out_shape=jax.ShapeDtypeStruct((cols, levels, 128), F32),
        in_specs=[sspec(), vspec(), vspec()],
        out_specs=vspec(),
        compiler_params=params(12),
        name="finish",
    )(place, own, other)


def local(anomalies, taper, obs_row, obs_col, obs_level, obs_value):
    members, levels, cols, lat_rows = anomalies.shape
    bands = lax.axis_size("lat")
    blocks = lax.axis_size("lon")
    mem, lat, lon = lax.axis_index("mem"), lax.axis_index("lat"), lax.axis_index("lon")
    coefs = cols * blocks
    lat_total = lat_rows * bands
    padded = -(-cols // 32) * 32
    half = padded // 2
    ensemble = members * lax.axis_size("mem")
    place = jnp.stack([mem, lat, lon // RING, lon % RING]).astype(jnp.int32)

    by_round = jnp.transpose(anomalies, (0, 2, 1, 3)).reshape(members // bands, bands, cols, levels, lat_rows)
    pair_out, early = lax.optimization_barrier((relayout(by_round, True, padded), place))
    pair = over_all(pair_out)
    last = over_all(relayout(by_round, False, padded))

    blocks_out = spread(early, obs_row, obs_col, obs_level, obs_value, half, levels, cols)
    by_z = [blocks_out[0]] + [shift_z(blocks_out[s], s) for s in range(1, RING)]
    by_x = []
    for t in range(RING):
        column = jnp.concatenate([piece[t] for piece in by_z], axis=0)
        by_x.append(column if t == 0 else shift_x(column, t))

    n_half = lat_total // 2
    coef_rows = taper.shape[1]
    taper_own = lax.dynamic_slice_in_dim(taper[0], mem * n_half, n_half, axis=1).astype(BF)
    payload = jnp.concatenate(by_x + [taper_own[:, :128], taper_own[:, 128:]], axis=0)
    own = jnp.stack([payload] + [shift_lat(payload, u) for u in range(1, RING)])
    other = swap(own)
    innov, weights = arrange(place, own, other, half, blocks, padded, coef_rows)

    tables = bases(cols, blocks, padded, lat_total)
    dims = (cols, blocks, bands, padded, coefs, lat_total)
    summed = member(place, pair, innov, weights, tables, None, False, dims)
    mine, theirs = member(place, last, innov, weights, tables, summed, True, dims)
    merged = (mine + swap(theirs).astype(F32)).astype(BF)
    pieces = over_all(merged)
    out = finish(place, pieces, swap(pieces), levels, cols, half, 1.0 / (ensemble - 1))
    return jnp.transpose(out, (1, 0, 2))


def solution(mesh):
    in_specs = (
        P("mem", None, "lon", "lat"),
        P("lon", "lat", None),
        P("lat", "lon"),
        P("lat", "lon"),
        P("lat", "lon"),
        P("lat", "lon"),
    )
    out_specs = P(None, "lon", "lat")

    return jax.shard_map(local, mesh=mesh, in_specs=in_specs, out_specs=out_specs, check_vma=False)
```

time: 235 us -> 184 us (0.78)
  blocking collectives: 50.8 us -> 24.8 us
  Pallas kernels: 69.4 us -> 54.3 us
  local copies, waits for them, and re-layouts: 28.5 us -> 15.2 us
  starting transfers between devices: 33.6 us -> 37.2 us
    ppermute x3 -> x12, waiting for transfers between devices: 2.28 us -> 50.4 us  [the longest x3 32.5 us: shift_x(): lax.ppermute(x, 'lon', [(z * RING + i, z * RING + (i + s) % RING) for z i...]
    all_to_all x4 -> x2, waiting for transfers between devices: 47.3 us -> 0.01 us  [over_all(): return lax.all_to_all(x, LL, split_axis=0, concat_axis=0, tiled=True)]
    all_gather x2 -> x0, blocking collectives: 27.9 us -> none  [the longest x1 24.3 us: local(): taper_own = lax.all_gather(taper_own, 'lat', axis=0, tiled=True)]
    ppermute x3 -> x12, starting transfers between devices: 6.48 us -> 20 us  [the longest x3 6.56 us: shift_z(): lax.ppermute(x, 'lon', [(z * RING + i, (z + s) % RING * RING + i) for z i...]
    pallas_call x3 -> x2, Pallas kernels: 43.1 us -> 30.6 us  [member(): pl.pallas_call(lambda *refs: member_kernel(*refs, first=first, final=fina...]
    slice x6 -> x0, local copies, waits for them, and re-layouts: 12.1 us -> none  [the longest x4 12.1 us: local(): anomalies[i:i + bands].reshape(bands * levels, cols, lat_rows)]
    all_to_all x4 -> x2, starting transfers between devices: 27.1 us -> 17.2 us  [over_all(): return lax.all_to_all(x, LL, split_axis=0, concat_axis=0, tiled=True)]
    pallas_call x1, Pallas kernels: 19.8 us -> 10.2 us  [bases(): pl.pallas_call(lambda *refs: basis_kernel(*refs, cols=cols, blocks=blocks...]
  transfers between devices with their start and end apart: 7 -> 14, of which waited for: 4 -> 6; matrix products, arithmetic and copies ran while one was open for 5% -> 1% of each run, Pallas kernels for 21% -> 18%
where the time goes in v1:
time: 184 us
  Pallas kernels  54.3 us (30%)
  waiting for transfers between devices  50.4 us (27%)
  starting transfers between devices  37.2 us (20%)
  blocking collectives  24.8 us (13%)
  local copies, waits for them, and re-layouts  15.2 us (8%)
    ppermute x3, waiting for transfers between devices, shift_x(): lax.ppermute(x, 'lon', [(z * RING + i, z * RING + (i + s) % RING) for z i...  32.5 us
    pallas_call x2, Pallas kernels, member(): pl.pallas_call(lambda *refs: member_kernel(*refs, first=first, final=fina...  30.6 us
    all_to_all x1, blocking collectives, over_all(): return lax.all_to_all(x, LL, split_axis=0, concat_axis=0, tiled=True)  24.8 us
    all_to_all x2, starting transfers between devices, over_all(): return lax.all_to_all(x, LL, split_axis=0, concat_axis=0, tiled=True)  17.2 us
    unnamed x38, local copies, waits for them, and re-layouts  15.1 us
    ppermute x3, waiting for transfers between devices, shift_lat(): return lax.ppermute(x, 'lat', [(i, (i + s) % RING) for i in range(RING)])  14 us
    pallas_call x1, Pallas kernels, bases(): pl.pallas_call(lambda *refs: basis_kernel(*refs, cols=cols, blocks=blocks...  10.2 us
    ppermute x3, starting transfers between devices, shift_z(): lax.ppermute(x, 'lon', [(z * RING + i, (z + s) % RING * RING + i) for z i...  6.56 us
  transfers between devices with their start and end apart: 14, of which 6 were waited for; matrix products, arithmetic and copies ran while one was open for 1% of the time, Pallas kernels for 18%

profile of v1, /device:TPU:1, one launch (start us, length us, event | category | flops | bytes accessed | tf_op | source)
XLA Modules:
  0.0 183.9 jit_solution(15776046094165320572)
XLA Ops:
  0.0 0.0 copy-start
  0.0 2.3 %copy-done.1 = bf16[12,16,90,128]{3,1,2,0:T(8,128)(2,1)S(1)} copy-done((bf16[12,16,90,128]{3,1,2,0:T(8,128)(2,1)S(1)}, bf16[12,16,90,128]{3,1,2,0:T(8,128)(2,1)}, u32[]{:S(2)}) %copy-start.1) | copy-done | bytes 4423704
  2.3 0.0 copy-start.4
  2.3 0.0 copy-start.5
  2.3 0.0 copy-start.6
  2.3 0.0 copy-start.7
  2.3 1.8 relayout_pair.1
  4.1 0.0 copy-start.3
  4.1 1.6 copy-done.3
  5.7 0.1 pad_add_fusion.refs_0_
  5.8 0.0 copy-done.4
  5.8 0.0 copy-done.5
  5.8 0.0 copy-done.6
  5.8 0.0 copy-done.7
  5.8 5.8 %spread.1 = bf16[4,4,48,128]{3,2,1,0:T(8,128)(2,1)S(1)} custom-call(s32[4]{0:T(128)S(1)} %pad_add_fusion.refs_0_, s32[64,128]{1,0:T(8,128)S(1)} %copy-done.4, s32[64,128]{1,0:T(8,128)S(1)} %copy-done.5, s32[64,128]{1,0:T(8,128)S(1)} %copy-done.6, f32[64,128]{1,0:T(8,128)S(1)} %copy-done.7), custom_call_target="tpu_custom_call" | custom-call | flops 6000000000 | bytes 1048576 | tf_op jit(solution)/shard_map/spread/pallas_call | solution.py:149
  11.6 2.5 %collective-permute-start = (bf16[4,48,128]{2,1,0:T(8,128)(2,1)S(1)}, bf16[4,48,128]{2,1,0:T(8,128)(2,1)S(1)}, u32[]{:S(2)}, u32[]{:S(2)}) collective-permute-start(bf16[4,48,128]{2,1,0:T(8,128)(2,1)S(1)} %get-tuple-element.30), channel_id=1, source_target_pairs={{0,8},{2,10},{4,12},{6,14},{8,16},{10,18},{12,20},{14,22},{16,24},... | collective-permute-start | bytes 147464 | tf_op jit(solution)/shard_map/ppermute | solution.py:43
  14.2 3.3 %collective-permute-start.1 = (bf16[4,48,128]{2,1,0:T(8,128)(2,1)S(1)}, bf16[4,48,128]{2,1,0:T(8,128)(2,1)S(1)}, u32[]{:S(2)}, u32[]{:S(2)}) collective-permute-start(bf16[4,48,128]{2,1,0:T(8,128)(2,1)S(1)} %get-tuple-element.29), channel_id=1, source_target_pairs={{0,16},{2,18},{4,20},{6,22},{8,24},{10,26},{12,28},{14,30},{16,0},... | collective-permute-start | bytes 147464 | tf_op jit(solution)/shard_map/ppermute | solution.py:43
  17.5 0.7 collective-permute-start.2
  18.2 8.3 %all-to-all-start.1 = ((bf16[64,2,96,128]{3,2,1,0:T(8,128)(2,1)}), bf16[64,2,96,128]{3,2,1,0:T(8,128)(2,1)}, u32[]{:S(2)}, u32[]{:S(2)}) async-start(bf16[64,2,96,128]{3,2,1,0:T(8,128)(2,1)} %copy-done.3), calls=%async_computation.1 | async-start | bytes 6291456 | tf_op jit(solution)/shard_map/all_to_all | solution.py:35
  26.6 0.0 copy-done
  26.6 0.0 copy-start.2
  26.6 0.0 collective-permute-done
  26.7 0.0 collective-permute-done.1
  26.7 0.0 collective-permute-done.2
  26.7 2.2 %collective-permute-start.5 = (bf16[192,128]{1,0:T(8,128)(2,1)S(1)}, bf16[192,128]{1,0:T(8,128)(2,1)S(1)}, u32[]{:S(2)}, u32[]{:S(2)}) collective-permute-start(bf16[192,128]{1,0:T(8,128)(2,1)S(1)} %pad_maximum_fusion.3), channel_id=1, source_target_pairs={{0,6},{2,0},{4,2},{6,4},{8,14},{10,8},{12,10},{14,12},{16,22},{18,... | collective-permute-start | bytes 147464 | tf_op jit(solution)/shard_map/ppermute | solution.py:49
  29.0 0.6 collective-permute-start.4
  29.5 0.6 collective-permute-start.3
  30.1 32.5 %collective-permute-done.3 = bf16[192,128]{1,0:T(8,128)(2,1)S(1)} collective-permute-done((bf16[192,128]{1,0:T(8,128)(2,1)S(1)}, bf16[192,128]{1,0:T(8,128)(2,1)S(1)}, u32[]{:S(2)}, u32[]{:S(2)}) %collective-permute-start.3) | collective-permute-done | bytes 49184 | tf_op jit(solution)/shard_map/ppermute | solution.py:49
  62.6 0.0 collective-permute-done.4
  62.7 0.0 collective-permute-done.5
  62.7 1.3 collective-permute-start.6
  64.0 2.6 %collective-permute-start.7 = (bf16[1488,128]{1,0:T(8,128)(2,1)S(1)}, bf16[1488,128]{1,0:T(8,128)(2,1)S(1)}, u32[]{:S(2)}, u32[]{:S(2)}) collective-permute-start(bf16[1488,128]{1,0:T(8,128)(2,1)S(1)} %slice_dynamic-update-slice_fusion), channel_id=1, source_target_pairs={{0,64},{32,96},{64,0},{96,32},{1,65},{33,97},{65,1},{97,33},{2,66}... | collective-permute-start | bytes 1142792 | tf_op jit(solution)/shard_map/ppermute | solution.py:39
  66.6 1.1 collective-permute-start.8
  67.7 3.5 %collective-permute-done.6 = bf16[1488,128]{1,0:T(8,128)(2,1)S(1)} collective-permute-done((bf16[1488,128]{1,0:T(8,128)(2,1)S(1)}, bf16[1488,128]{1,0:T(8,128)(2,1)S(1)}, u32[]{:S(2)}, u32[]{:S(2)}) %collective-permute-start.6) | collective-permute-done | bytes 380960 | tf_op jit(solution)/shard_map/ppermute | solution.py:39
  71.2 9.3 %collective-permute-done.7 = bf16[1488,128]{1,0:T(8,128)(2,1)S(1)} collective-permute-done((bf16[1488,128]{1,0:T(8,128)(2,1)S(1)}, bf16[1488,128]{1,0:T(8,128)(2,1)S(1)}, u32[]{:S(2)}, u32[]{:S(2)}) %collective-permute-start.7) | collective-permute-done | bytes 380960 | tf_op jit(solution)/shard_map/ppermute | solution.py:39
  80.5 1.2 collective-permute-done.8
  81.7 1.3 pad_maximum_fusion.refs_1_
  83.1 2.9 %collective-permute-start.9 = (bf16[4,1488,128]{2,1,0:T(8,128)(2,1)}, bf16[4,1488,128]{2,1,0:T(8,128)(2,1)}, u32[]{:S(2)}, u32[]{:S(2)}) collective-permute-start(bf16[4,1488,128]{2,1,0:T(8,128)(2,1)} %pad_maximum_fusion.refs_1_), channel_id=1, source_target_pairs={{0,1},{1,0},{2,3},{3,2},{4,5},{5,4},{6,7},{7,6},{8,9},{9,8},{10,11... | collective-permute-start | bytes 4571144 | tf_op jit(solution)/shard_map/ppermute | solution.py:55
  85.9 0.0 copy-done.2
  85.9 1.7 relayout_last.1
  87.6 0.0 all-to-all-done.1.refs_1_
  87.6 8.9 %all-to-all-start = ((bf16[64,1,96,128]{3,2,1,0:T(8,128)(2,1)}), bf16[64,1,96,128]{3,2,1,0:T(8,128)(2,1)S(1)}, u32[]{:S(2)}, u32[]{:S(2)}) async-start(bf16[64,1,96,128]{3,2,1,0:T(8,128)(2,1)} %relayout_last.1), calls=%async_computation | async-start | bytes 3145728 | tf_op jit(solution)/shard_map/all_to_all | solution.py:35
  96.5 10.2 %bases.1 = (bf16[1536,1536]{1,0:T(8,128)(2,1)S(1)}, bf16[1536,1536]{1,0:T(8,128)(2,1)S(1)}, bf16[512,512]{1,0:T(8,128)(2,1)S(1)}, bf16[512,512]{1,0:T(8,128)(2,1)S(1)}) custom-call(), custom_call_target="tpu_custom_call" | custom-call | flops 12000000000 | bytes 1048576 | tf_op jit(solution)/shard_map/bases/pallas_call | solution.py:233
  106.7 0.0 copy-start.12
  106.7 2.1 %copy-done.12 = bf16[1536,1536]{1,0:T(8,128)(2,1)} copy-done((bf16[1536,1536]{1,0:T(8,128)(2,1)}, bf16[1536,1536]{1,0:T(8,128)(2,1)S(1)}, u32[]{:S(2)}) %copy-start.12) | copy-done | bytes 4718616
  108.8 2.2 %copy-done.13 = bf16[1536,1536]{1,0:T(8,128)(2,1)} copy-done((bf16[1536,1536]{1,0:T(8,128)(2,1)}, bf16[1536,1536]{1,0:T(8,128)(2,1)S(1)}, u32[]{:S(2)}) %copy-start.13) | copy-done | bytes 4718616
  111.0 0.0 collective-permute-done.9.refs_2_
  111.0 2.2 %arrange.1 = (bf16[64,96,128]{2,1,0:T(8,128)(2,1)S(1)}, bf16[4,1440,128]{2,1,0:T(8,128)(2,1)S(1)}) custom-call(s32[4]{0:T(128)S(1)} %pad_add_fusion.refs_0_, bf16[4,1488,128]{2,1,0:T(8,128)(2,1)} %pad_maximum_fusion.refs_1_, bf16[4,1488,128]{2,1,0:T(8,128)(2,1)} %collective-permute-done.9.refs_2_), custom_call_target="tpu_custom_call" | custom-call | flops 1000000000 | bytes 1048576 | tf_op jit(solution)/shard_map/arrange/pallas_call | solution.py:267
  113.2 19.8 %member_pair.1.refs_8_ = f32[64,96,128]{2,1,0:T(8,128)S(1)} custom-call(s32[4]{0:T(128)S(1)} %pad_add_fusion.refs_0_, bf16[64,2,96,128]{3,2,1,0:T(8,128)(2,1)} %all-to-all-done.1.refs_1_, bf16[64,96,128]{2,1,0:T(8,128)(2,1)S(1)} %get-tuple-element.16.refs_2_, bf16[4,1440,128]{2,1,0:T(8,128)(2,1)S(1)} %get-tuple-element.17.refs_3_, ...), custom_call_target="tpu_custom_call" | custom-call | flops 12000000000 | bytes 1048576 | tf_op jit(solution)/shard_map/member_pair/pallas_call | solution.py:388
  133.1 0.0 copy-start.8
  133.1 1.2 copy-done.8
  134.2 1.1 copy-done.10
  135.3 1.7 copy-done.14
  137.0 0.0 all-to-all-done.refs_1_
  137.0 1.4 copy-done.9
  138.4 1.4 copy-done.11
  139.8 10.7 %member_last.1 = (f32[64,48,128]{2,1,0:T(8,128)S(1)}, bf16[64,48,128]{2,1,0:T(8,128)(2,1)S(1)}) custom-call(s32[4]{0:T(128)S(1)} %pad_add_fusion.refs_0_, bf16[64,1,96,128]{3,2,1,0:T(8,128)(2,1)S(1)} %all-to-all-done.refs_1_, bf16[64,96,128]{2,1,0:T(8,128)(2,1)S(1)} %copy-done.9, bf16[4,1440,128]{2,1,0:T(8,128)(2,1)S(1)} %copy-done.11, ...), custom_call_target="tpu_custom_call" | custom-call | flops 6000000000 | bytes 1048576 | tf_op jit(solution)/shard_map/member_last/pallas_call | solution.py:388
  150.6 0.4 collective-permute-start.10
  150.9 2.0 %collective-permute-done.10 = bf16[64,48,128]{2,1,0:T(8,128)(2,1)S(1)} collective-permute-done((bf16[64,48,128]{2,1,0:T(8,128)(2,1)S(1)}, bf16[64,48,128]{2,1,0:T(8,128)(2,1)S(1)}, u32[]{:S(2)}, u32[]{:S(2)}) %collective-permute-start.10) | collective-permute-done | bytes 786464 | tf_op jit(solution)/shard_map/ppermute | solution.py:55
  152.9 0.2 add_convert_fusion
  153.1 24.8 %all_to_all.15.refs_1_ = bf16[64,48,128]{2,1,0:T(8,128)(2,1)S(1)} all-to-all(bf16[64,48,128]{2,1,0:T(8,128)(2,1)S(1)} %add_convert_fusion), channel_id=1, replica_groups=mesh['lat'=4,'lon'=16,'mem'=2] {'lat','lon'}, dimensions={0} | all-to-all | bytes 1572864 | tf_op jit(solution)/shard_map/all_to_all | solution.py:35
  177.9 1.9 %collective-permute-start.11 = (bf16[64,48,128]{2,1,0:T(8,128)(2,1)S(1)}, bf16[64,48,128]{2,1,0:T(8,128)(2,1)S(1)}, u32[]{:S(2)}, u32[]{:S(2)}) collective-permute-start(bf16[64,48,128]{2,1,0:T(8,128)(2,1)S(1)} %all_to_all.15.refs_1_), channel_id=1, source_target_pairs={{0,1},{1,0},{2,3},{3,2},{4,5},{5,4},{6,7},{7,6},{8,9},{9,8},{10,11... | collective-permute-start | bytes 2359304 | tf_op jit(solution)/shard_map/ppermute | solution.py:55
  179.8 1.9 %collective-permute-done.11.refs_2_ = bf16[64,48,128]{2,1,0:T(8,128)(2,1)S(1)} collective-permute-done((bf16[64,48,128]{2,1,0:T(8,128)(2,1)S(1)}, bf16[64,48,128]{2,1,0:T(8,128)(2,1)S(1)}, u32[]{:S(2)}, u32[]{:S(2)}) %collective-permute-start.11) | collective-permute-done | bytes 786464 | tf_op jit(solution)/shard_map/ppermute | solution.py:55
  181.7 2.1 %finish.1 = f32[90,16,128]{2,1,0:T(8,128)} custom-call(s32[4]{0:T(128)S(1)} %pad_add_fusion.refs_0_, bf16[64,48,128]{2,1,0:T(8,128)(2,1)S(1)} %all_to_all.15.refs_1_, bf16[64,48,128]{2,1,0:T(8,128)(2,1)S(1)} %collective-permute-done.11.refs_2_), custom_call_target="tpu_custom_call" | custom-call | tf_op jit(solution)/shard_map/finish/pallas_call | solution.py:415
  (24 shorter events, 0.2 us)
Async XLA Ops:
  0.0 26.6 %copy-start = (f32[1,360,512]{2,1,0:T(8,128)S(1)}, f32[1,360,512]{2,1,0:T(8,128)}, u32[]{:S(2)}) copy-start(f32[1,360,512]{2,1,0:T(8,128)} %param.7) | copy-start | bytes 2211844
  0.0 2.3 %copy-start.1 = (bf16[12,16,90,128]{3,1,2,0:T(8,128)(2,1)S(1)}, bf16[12,16,90,128]{3,1,2,0:T(8,128)(2,1)}, u32[]{:S(2)}) copy-start(bf16[12,16,90,128]{3,1,2,0:T(8,128)(2,1)} %param.6) | copy-start | bytes 13271044
  2.3 3.5 %copy-start.4 = (s32[64,128]{1,0:T(8,128)S(1)}, s32[64,128]{1,0:T(8,128)}, u32[]{:S(2)}) copy-start(s32[64,128]{1,0:T(8,128)} %refs_1_.1) | copy-start | bytes 98308
  2.3 3.5 %copy-start.5 = (s32[64,128]{1,0:T(8,128)S(1)}, s32[64,128]{1,0:T(8,128)}, u32[]{:S(2)}) copy-start(s32[64,128]{1,0:T(8,128)} %refs_2_.1) | copy-start | bytes 98308
  2.3 3.5 %copy-start.6 = (s32[64,128]{1,0:T(8,128)S(1)}, s32[64,128]{1,0:T(8,128)}, u32[]{:S(2)}) copy-start(s32[64,128]{1,0:T(8,128)} %refs_3_.1) | copy-start | bytes 98308
  2.3 3.5 %copy-start.7 = (f32[64,128]{1,0:T(8,128)S(1)}, f32[64,128]{1,0:T(8,128)}, u32[]{:S(2)}) copy-start(f32[64,128]{1,0:T(8,128)} %refs_4_.1) | copy-start | bytes 98308
  4.1 1.6 copy-start.3
  11.6 15.0 %collective-permute-start = (bf16[4,48,128]{2,1,0:T(8,128)(2,1)S(1)}, bf16[4,48,128]{2,1,0:T(8,128)(2,1)S(1)}, u32[]{:S(2)}, u32[]{:S(2)}) collective-permute-start(bf16[4,48,128]{2,1,0:T(8,128)(2,1)S(1)} %get-tuple-element.30), channel_id=1, source_target_pairs={{0,8},{2,10},{4,12},{6,14},{8,16},{10,18},{12,20},{14,22},{16,24},... | collective-permute-start | bytes 147464 | tf_op jit(solution)/shard_map/ppermute | solution.py:43
  14.2 12.5 %collective-permute-start.1 = (bf16[4,48,128]{2,1,0:T(8,128)(2,1)S(1)}, bf16[4,48,128]{2,1,0:T(8,128)(2,1)S(1)}, u32[]{:S(2)}, u32[]{:S(2)}) collective-permute-start(bf16[4,48,128]{2,1,0:T(8,128)(2,1)S(1)} %get-tuple-element.29), channel_id=1, source_target_pairs={{0,16},{2,18},{4,20},{6,22},{8,24},{10,26},{12,28},{14,30},{16,0},... | collective-permute-start | bytes 147464 | tf_op jit(solution)/shard_map/ppermute | solution.py:43
  17.5 9.2 %collective-permute-start.2 = (bf16[4,48,128]{2,1,0:T(8,128)(2,1)S(1)}, bf16[4,48,128]{2,1,0:T(8,128)(2,1)S(1)}, u32[]{:S(2)}, u32[]{:S(2)}) collective-permute-start(bf16[4,48,128]{2,1,0:T(8,128)(2,1)S(1)} %get-tuple-element.28), channel_id=1, source_target_pairs={{0,24},{2,26},{4,28},{6,30},{8,0},{10,2},{12,4},{14,6},{16,8},{18,... | collective-permute-start | bytes 147464 | tf_op jit(solution)/shard_map/ppermute | solution.py:43
  18.2 69.4 %all-to-all-start.1 = ((bf16[64,2,96,128]{3,2,1,0:T(8,128)(2,1)}), bf16[64,2,96,128]{3,2,1,0:T(8,128)(2,1)}, u32[]{:S(2)}, u32[]{:S(2)}) async-start(bf16[64,2,96,128]{3,2,1,0:T(8,128)(2,1)} %copy-done.3), calls=%async_computation.1 | async-start | bytes 6291456 | tf_op jit(solution)/shard_map/all_to_all | solution.py:35
  26.6 59.3 %copy-start.2 = (bf16[12,16,90,128]{3,1,2,0:T(8,128)(2,1)S(1)}, bf16[12,16,90,128]{3,1,2,0:T(8,128)(2,1)}, u32[]{:S(2)}) copy-start(bf16[12,16,90,128]{3,1,2,0:T(8,128)(2,1)} %param.6) | copy-start | bytes 13271044
  26.7 35.9 %collective-permute-start.5 = (bf16[192,128]{1,0:T(8,128)(2,1)S(1)}, bf16[192,128]{1,0:T(8,128)(2,1)S(1)}, u32[]{:S(2)}, u32[]{:S(2)}) collective-permute-start(bf16[192,128]{1,0:T(8,128)(2,1)S(1)} %pad_maximum_fusion.3), channel_id=1, source_target_pairs={{0,6},{2,0},{4,2},{6,4},{8,14},{10,8},{12,10},{14,12},{16,22},{18,... | collective-permute-start | bytes 147464 | tf_op jit(solution)/shard_map/ppermute | solution.py:49
  29.0 33.7 %collective-permute-start.4 = (bf16[192,128]{1,0:T(8,128)(2,1)S(1)}, bf16[192,128]{1,0:T(8,128)(2,1)S(1)}, u32[]{:S(2)}, u32[]{:S(2)}) collective-permute-start(bf16[192,128]{1,0:T(8,128)(2,1)S(1)} %pad_maximum_fusion.2), channel_id=1, source_target_pairs={{0,4},{2,6},{4,0},{6,2},{8,12},{10,14},{12,8},{14,10},{16,20},{18,... | collective-permute-start | bytes 147464 | tf_op jit(solution)/shard_map/ppermute | solution.py:49
  29.5 33.1 %collective-permute-start.3 = (bf16[192,128]{1,0:T(8,128)(2,1)S(1)}, bf16[192,128]{1,0:T(8,128)(2,1)S(1)}, u32[]{:S(2)}, u32[]{:S(2)}) collective-permute-start(bf16[192,128]{1,0:T(8,128)(2,1)S(1)} %pad_maximum_fusion.1), channel_id=1, source_target_pairs={{0,2},{2,4},{4,6},{6,0},{8,10},{10,12},{12,14},{14,8},{16,18},{18,... | collective-permute-start | bytes 147464 | tf_op jit(solution)/shard_map/ppermute | solution.py:49
  62.7 8.5 %collective-permute-start.6 = (bf16[1488,128]{1,0:T(8,128)(2,1)S(1)}, bf16[1488,128]{1,0:T(8,128)(2,1)S(1)}, u32[]{:S(2)}, u32[]{:S(2)}) collective-permute-start(bf16[1488,128]{1,0:T(8,128)(2,1)S(1)} %slice_dynamic-update-slice_fusion), channel_id=1, source_target_pairs={{0,32},{32,64},{64,96},{96,0},{1,33},{33,65},{65,97},{97,1},{2,34}... | collective-permute-start | bytes 1142792 | tf_op jit(solution)/shard_map/ppermute | solution.py:39
  64.0 16.5 %collective-permute-start.7 = (bf16[1488,128]{1,0:T(8,128)(2,1)S(1)}, bf16[1488,128]{1,0:T(8,128)(2,1)S(1)}, u32[]{:S(2)}, u32[]{:S(2)}) collective-permute-start(bf16[1488,128]{1,0:T(8,128)(2,1)S(1)} %slice_dynamic-update-slice_fusion), channel_id=1, source_target_pairs={{0,64},{32,96},{64,0},{96,32},{1,65},{33,97},{65,1},{97,33},{2,66}... | collective-permute-start | bytes 1142792 | tf_op jit(solution)/shard_map/ppermute | solution.py:39
  66.6 15.1 %collective-permute-start.8 = (bf16[1488,128]{1,0:T(8,128)(2,1)S(1)}, bf16[1488,128]{1,0:T(8,128)(2,1)S(1)}, u32[]{:S(2)}, u32[]{:S(2)}) collective-permute-start(bf16[1488,128]{1,0:T(8,128)(2,1)S(1)} %slice_dynamic-update-slice_fusion), channel_id=1, source_target_pairs={{0,96},{32,0},{64,32},{96,64},{1,97},{33,1},{65,33},{97,65},{2,98}... | collective-permute-start | bytes 1142792 | tf_op jit(solution)/shard_map/ppermute | solution.py:39
  83.1 28.0 %collective-permute-start.9 = (bf16[4,1488,128]{2,1,0:T(8,128)(2,1)}, bf16[4,1488,128]{2,1,0:T(8,128)(2,1)}, u32[]{:S(2)}, u32[]{:S(2)}) collective-permute-start(bf16[4,1488,128]{2,1,0:T(8,128)(2,1)} %pad_maximum_fusion.refs_1_), channel_id=1, source_target_pairs={{0,1},{1,0},{2,3},{3,2},{4,5},{5,4},{6,7},{7,6},{8,9},{9,8},{10,11... | collective-permute-start | bytes 4571144 | tf_op jit(solution)/shard_map/ppermute | solution.py:55
  87.6 49.4 %all-to-all-start = ((bf16[64,1,96,128]{3,2,1,0:T(8,128)(2,1)}), bf16[64,1,96,128]{3,2,1,0:T(8,128)(2,1)S(1)}, u32[]{:S(2)}, u32[]{:S(2)}) async-start(bf16[64,1,96,128]{3,2,1,0:T(8,128)(2,1)} %relayout_last.1), calls=%async_computation | async-start | bytes 3145728 | tf_op jit(solution)/shard_map/all_to_all | solution.py:35
  106.7 2.2 %copy-start.12 = (bf16[1536,1536]{1,0:T(8,128)(2,1)}, bf16[1536,1536]{1,0:T(8,128)(2,1)S(1)}, u32[]{:S(2)}) copy-start(bf16[1536,1536]{1,0:T(8,128)(2,1)S(1)} %get-tuple-element.18.refs_4_) | copy-start | bytes 14155780
  108.8 2.2 %copy-start.13 = (bf16[1536,1536]{1,0:T(8,128)(2,1)}, bf16[1536,1536]{1,0:T(8,128)(2,1)S(1)}, u32[]{:S(2)}) copy-start(bf16[1536,1536]{1,0:T(8,128)(2,1)S(1)} %get-tuple-element.19.refs_5_) | copy-start | bytes 14155780
  133.1 1.2 copy-start.8
  134.2 1.1 copy-start.10
  135.3 1.7 copy-start.14
  137.0 1.4 copy-start.9
  138.4 1.4 copy-start.11
  150.6 2.4 %collective-permute-start.10 = (bf16[64,48,128]{2,1,0:T(8,128)(2,1)S(1)}, bf16[64,48,128]{2,1,0:T(8,128)(2,1)S(1)}, u32[]{:S(2)}, u32[]{:S(2)}) collective-permute-start(bf16[64,48,128]{2,1,0:T(8,128)(2,1)S(1)} %get-tuple-element.24), channel_id=1, source_target_pairs={{0,1},{1,0},{2,3},{3,2},{4,5},{5,4},{6,7},{7,6},{8,9},{9,8},{10,11... | collective-permute-start | bytes 2359304 | tf_op jit(solution)/shard_map/ppermute | solution.py:55
  177.9 3.8 %collective-permute-start.11 = (bf16[64,48,128]{2,1,0:T(8,128)(2,1)S(1)}, bf16[64,48,128]{2,1,0:T(8,128)(2,1)S(1)}, u32[]{:S(2)}, u32[]{:S(2)}) collective-permute-start(bf16[64,48,128]{2,1,0:T(8,128)(2,1)S(1)} %all_to_all.15.refs_1_), channel_id=1, source_target_pairs={{0,1},{1,0},{2,3},{3,2},{4,5},{5,4},{6,7},{7,6},{8,9},{9,8},{10,11... | collective-permute-start | bytes 2359304 | tf_op jit(solution)/shard_map/ppermute | solution.py:55

commit v2 on v1

--- a/solution.py
+++ b/solution.py
@@ -39,23 +39,12 @@
     return lax.ppermute(x, "lat", [(i, (i + s) % RING) for i in range(RING)])
 
 
-def shift_z(x, s):
-    return lax.ppermute(
-        x, "lon", [(z * RING + i, (z + s) % RING * RING + i) for z in range(RING) for i in range(RING)]
-    )
-
-
-def shift_x(x, s):
-    return lax.ppermute(
-        x, "lon", [(z * RING + i, z * RING + (i + s) % RING) for z in range(RING) for i in range(RING)]
-    )
-
-
 def swap(x):
     return lax.ppermute(x, "mem", SWAP)
 
 
-def relayout_kernel(in_ref, out_ref, *, split, cols, levels, padded):
+def relayout_kernel(in_ref, extra, out_ref, *, cols, levels, padded):
+    split = extra is not None
     size = 16 * levels
     to = lax.broadcasted_iota(jnp.int32, (size, size), 0)
     frm = lax.broadcasted_iota(jnp.int32, (size, size), 1)
@@ -74,39 +63,47 @@
             for p in range(2):
                 piece = turned[16 * l : 16 * l + 16, 128 * p : 128 * p + 128]
                 if split:
-                    out_ref[l, p, start : start + 16, :] = piece
+                    out_ref[l, p * padded + start : p * padded + start + 16, :] = piece
                 else:
-                    out_ref[p * levels + l, 0, start : start + 16, :] = piece
-
-
-def relayout(fields, pair, padded):
+                    out_ref[p * levels + l, start : start + 16, :] = piece
+    if split:
+        out_ref[:, 2 * padded :, :] = extra[...]
+
+
+def relayout_pair(fields, extra, padded):
+    _, bands, cols, levels, lanes = fields.shape
+    rows = 2 * padded + extra.shape[1]
+    return pl.pallas_call(
+        lambda i, e, o: relayout_kernel(i, e, o, cols=cols, levels=levels, padded=padded),
+        grid=(bands,),
+        in_specs=[
+            pl.BlockSpec((2, 1, cols, levels, lanes), lambda g: (0, g, 0, 0, 0)),
+            pl.BlockSpec(extra.shape, lambda g: (0, 0, 0)),
+        ],
+        out_specs=pl.BlockSpec((levels, rows, lanes), lambda g: (g, 0, 0)),
+        out_shape=jax.ShapeDtypeStruct((bands * levels, rows, lanes), BF),
+        compiler_params=params(58),
+        name="relayout_pair",
+    )(fields, extra)
+
+
+def relayout_last(fields, padded):
     rounds, bands, cols, levels, lanes = fields.shape
-    kernel = lambda i, o: relayout_kernel(i, o, split=pair, cols=cols, levels=levels, padded=padded)
-    if pair:
-        return pl.pallas_call(
-            kernel,
-            grid=(bands,),
-            in_specs=[pl.BlockSpec((2, 1, cols, levels, lanes), lambda g: (0, g, 0, 0, 0))],
-            out_specs=pl.BlockSpec((levels, 2, padded, lanes), lambda g: (g, 0, 0, 0)),
-            out_shape=jax.ShapeDtypeStruct((bands * levels, 2, padded, lanes), BF),
-            compiler_params=params(12),
-            name="relayout_pair",
-        )(fields)
-    return pl.pallas_call(
-        kernel,
+    return pl.pallas_call(
+        lambda i, o: relayout_kernel(i, None, o, cols=cols, levels=levels, padded=padded),
         grid=(bands // 2,),
         in_specs=[pl.BlockSpec((1, 2, cols, levels, lanes), lambda g: (rounds - 1, g, 0, 0, 0))],
-        out_specs=pl.BlockSpec((2 * levels, 1, padded, lanes), lambda g: (g, 0, 0, 0)),
-        out_shape=jax.ShapeDtypeStruct((bands * levels, 1, padded, lanes), BF),
-        compiler_params=params(12),
+        out_specs=pl.BlockSpec((2 * levels, padded, lanes), lambda g: (g, 0, 0)),
+        out_shape=jax.ShapeDtypeStruct((bands * levels, padded, lanes), BF),
+        compiler_params=params(58),
         name="relayout_last",
     )(fields)
 
 
 def spread_kernel(place, row_ref, col_ref, level_ref, value_ref, out_ref, acc, *, half, levels, cols):
-    mem, lat, z, x = place[0], place[1], place[2], place[3]
+    mem, lat, lon = place[0], place[1], place[2]
     slots = levels * half
-    col_start = (z * RING + x) * cols + mem * half
+    col_start = lon * cols + mem * half
     acc[...] = jnp.zeros_like(acc)
     slot_ids = lax.broadcasted_iota(jnp.int32, (slots, 128), 0)
     row_ids = lax.broadcasted_iota(jnp.int32, (128, 128), 0)
@@ -138,17 +135,13 @@
         return carry
 
     lax.fori_loop(0, row_ref.shape[0] // 8, add_group, 0)
-    for s in range(RING):
-        for t in range(RING):
-            level = lax.rem(z + s, RING) * RING + lax.rem(x + t, RING)
-            rows = pl.ds(pl.multiple_of(level * half, 8), half)
-            out_ref[s, t] = (acc[rows, :128] + acc[rows, 128:]).astype(BF)
+    out_ref[...] = (acc[:, :128] + acc[:, 128:]).astype(BF).reshape(levels, half, 128)
 
 
 def spread(place, obs_row, obs_col, obs_level, obs_value, half, levels, cols):
     return pl.pallas_call(
         lambda *refs: spread_kernel(*refs, half=half, levels=levels, cols=cols),
-        out_shape=jax.ShapeDtypeStruct((RING, RING, half, 128), BF),
+        out_shape=jax.ShapeDtypeStruct((levels, half, 128), BF),
         in_specs=[sspec()] + [vspec()] * 4,
         out_specs=vspec(),
         scratch_shapes=[pltpu.VMEM((levels * half, 256), F32)],
@@ -239,39 +232,28 @@
             jax.ShapeDtypeStruct((lat_total, lat_total), BF),
         ),
         out_specs=(vspec(),) * 4,
-        compiler_params=params(20),
+        compiler_params=params(58),
         cost_estimate=cost(12e9),
         name="bases",
     )()
 
 
-def arrange_kernel(place, own, other, innov, taper, *, half, blocks, rows_each):
-    mem, lat, z, x = place[0], place[1], place[2], place[3]
-    packed = blocks * half
+def arrange_kernel(place, own, other, taper, *, rows_each):
+    mem, lat = place[0], place[1]
     for ref, side in ((own, mem), (other, 1 - mem)):
-        rows = pl.ds(pl.multiple_of(side * half, 16), half)
         for u in range(RING):
-            band = lax.rem(lat + RING - u, RING)
-            for t in range(RING):
-                for s in range(RING):
-                    j = lax.rem(z + RING - s, RING) * RING + lax.rem(x + RING - t, RING)
-                    start = (t * RING + s) * half
-                    innov[band * blocks + j, rows, :] = ref[u, start : start + half, :]
-            into = pl.ds(pl.multiple_of(band * rows_each, 8), rows_each)
+            into = pl.ds(pl.multiple_of(lax.rem(lat + RING - u, RING) * rows_each, 8), rows_each)
             for q in range(2):
-                start = packed + q * rows_each
-                taper[2 * side + q, into, :] = ref[u, start : start + rows_each, :]
-
-
-def arrange(place, own, other, half, blocks, padded, rows_each):
-    return pl.pallas_call(
-        lambda *refs: arrange_kernel(*refs, half=half, blocks=blocks, rows_each=rows_each),
-        out_shape=(
-            jax.ShapeDtypeStruct((RING * blocks, padded, 128), BF),
-            jax.ShapeDtypeStruct((4, RING * rows_each, 128), BF),
-        ),
+                taper[2 * side + q, into, :] = ref[u, :, 128 * q : 128 * q + 128]
+
+
+def arrange(place, own, other):
+    rows_each = own.shape[1]
+    return pl.pallas_call(
+        lambda *refs: arrange_kernel(*refs, rows_each=rows_each),
+        out_shape=jax.ShapeDtypeStruct((4, RING * rows_each, 128), BF),
         in_specs=[sspec(), vspec(), vspec()],
-        out_specs=(vspec(), vspec()),
+        out_specs=vspec(),
         compiler_params=params(12),
         cost_estimate=cost(1e9),
         name="arrange",
@@ -279,8 +261,8 @@
 
 
 def member_kernel(*refs, first, final, blocks, bands, padded, coefs):
-    place, field, innov_hbm, taper_hbm, lon_hbm, lon_t_hbm, lat_hbm, lat_t_hbm = refs[:8]
-    rest = list(refs[8:])
+    place, field, pair_hbm, other_hbm, taper_hbm, lon_hbm, lon_t_hbm, lat_hbm, lat_t_hbm = refs[:9]
+    rest = list(refs[9:])
     so_far_hbm = None if first else rest.pop(0)
     if final:
         own_out, other_out, acc = rest[0], rest[1], rest.pop()
@@ -299,7 +281,14 @@
         copy.start()
         return copy
 
-    innov_copy = fetch(innov_hbm, innov)
+    half = padded // 2
+    mem = place[0]
+    own_rows = pl.ds(pl.multiple_of(mem * half, half), half)
+    other_rows = pl.ds(pl.multiple_of((1 - mem) * half, half), half)
+    innov_copies = [
+        fetch(pair_hbm.at[:, pl.ds(2 * padded, half), :], innov.at[:, own_rows, :]),
+        fetch(other_hbm, innov.at[:, other_rows, :]),
+    ]
     lon_t_copies = [fetch(lon_t_hbm.at[pl.ds(0, step)], lon_t_ref.at[pl.ds(0, step)])]
     lat_copies = [fetch(lat_hbm, lat_ref), fetch(taper_hbm, taper), fetch(lat_t_hbm, lat_t_ref)]
     lon_t_copies += [
@@ -311,14 +300,15 @@
     if not first:
         lon_copies.append(fetch(so_far_hbm, acc))
     inverse[coefs:, :] = jnp.zeros((wide - coefs, inverse.shape[1]), BF)
-    innov_copy.wait()
+    for copy in innov_copies:
+        copy.wait()
 
     def weigh(i):
         def body(j, carry):
             rows = pl.ds(pl.multiple_of(j * padded, padded), padded)
             for a in range(bands):
                 spot = a * blocks + j
-                weighted[rows, 128 * a : 128 * a + 128] = field[spot, i] * innov[spot]
+                weighted[rows, 128 * a : 128 * a + 128] = field[spot, i * padded : (i + 1) * padded, :] * innov[spot]
             return carry
 
         lax.fori_loop(0, blocks, body, 0)
@@ -340,13 +330,13 @@
                 for a in range(bands):
                     spot = a * blocks + b * group + g
                     piece = localized[g * padded : (g + 1) * padded, 128 * a : 128 * a + 128]
-                    piece = piece * field[spot, i].astype(F32)
+                    piece = piece * field[spot, i * padded : (i + 1) * padded, :].astype(F32)
                     acc[spot] = piece if first and i == 0 else piece + acc[spot]
             return carry
 
         lax.fori_loop(0, blocks // group, body, 0)
 
-    for i in range(field.shape[1]):
+    for i in range(field.shape[1] // padded):
         weigh(i)
         if i == 0:
             for copy in [lon_t_copies[0], *lat_copies]:
@@ -359,21 +349,20 @@
                 copy.wait()
         gridded(i)
     if final:
-        half = padded // 2
-        mem = place[0]
-        own_out[...] = acc[:, pl.ds(pl.multiple_of(mem * half, half), half), :]
-        other_out[...] = acc[:, pl.ds(pl.multiple_of((1 - mem) * half, half), half), :].astype(BF)
-
-
-def member(place, field, innov, taper, tables, so_far, final, dims):
+        own_out[...] = acc[:, own_rows, :]
+        other_out[...] = acc[:, other_rows, :].astype(BF)
+
+
+def member(place, field, pair, other, taper, tables, so_far, final, dims):
     _, blocks, bands, padded, coefs, lat_total = dims
     spots = bands * blocks
     half = padded // 2
     wide = padded * blocks
     first = so_far is None
-    far = [innov, taper, *tables] + ([] if first else [so_far])
+    far = [pair, other, taper, *tables] + ([] if first else [so_far])
     scratch = [pltpu.VMEM((wide, lat_total), BF), pltpu.VMEM((wide, lat_total), BF)]
-    scratch += [pltpu.VMEM(array.shape, array.dtype) for array in (innov, taper, *tables)]
+    scratch.append(pltpu.VMEM((spots, padded, 128), BF))
+    scratch += [pltpu.VMEM(array.shape, array.dtype) for array in (taper, *tables)]
     scratch.append(pltpu.SemaphoreType.DMA((16,)))
     if final:
         out_shape = (
@@ -393,8 +382,8 @@
         in_specs=[sspec(), vspec()] + [pl.BlockSpec(memory_space=pltpu.HBM)] * len(far),
         out_specs=out_specs,
         scratch_shapes=scratch,
-        compiler_params=params(44),
-        cost_estimate=cost(field.shape[1] * 6e9),
+        compiler_params=params(60),
+        cost_estimate=cost(field.shape[1] // padded * 6e9),
         name="member_last" if final else "member_pair",
     )(place, field, *far)
 
@@ -432,32 +421,28 @@
     padded = -(-cols // 32) * 32
     half = padded // 2
     ensemble = members * lax.axis_size("mem")
-    place = jnp.stack([mem, lat, lon // RING, lon % RING]).astype(jnp.int32)
+    place = jnp.stack([mem, lat, lon]).astype(jnp.int32)
+
+    n_half = lat_total // 2
+    taper_mine = lax.dynamic_slice_in_dim(taper[0], mem * n_half, n_half, axis=1).astype(BF)
+    ring = [taper_mine]
+    for u in range(1, RING):
+        ring.append(shift_lat(taper_mine, u))
+    innovation = spread(place, obs_row, obs_col, obs_level, obs_value, half, levels, cols)
 
     by_round = jnp.transpose(anomalies, (0, 2, 1, 3)).reshape(members // bands, bands, cols, levels, lat_rows)
-    pair_out, early = lax.optimization_barrier((relayout(by_round, True, padded), place))
+    pair_out = relayout_pair(by_round, innovation, padded)
     pair = over_all(pair_out)
-    last = over_all(relayout(by_round, False, padded))
-
-    blocks_out = spread(early, obs_row, obs_col, obs_level, obs_value, half, levels, cols)
-    by_z = [blocks_out[0]] + [shift_z(blocks_out[s], s) for s in range(1, RING)]
-    by_x = []
-    for t in range(RING):
-        column = jnp.concatenate([piece[t] for piece in by_z], axis=0)
-        by_x.append(column if t == 0 else shift_x(column, t))
-
-    n_half = lat_total // 2
-    coef_rows = taper.shape[1]
-    taper_own = lax.dynamic_slice_in_dim(taper[0], mem * n_half, n_half, axis=1).astype(BF)
-    payload = jnp.concatenate(by_x + [taper_own[:, :128], taper_own[:, 128:]], axis=0)
-    own = jnp.stack([payload] + [shift_lat(payload, u) for u in range(1, RING)])
-    other = swap(own)
-    innov, weights = arrange(place, own, other, half, blocks, padded, coef_rows)
+    last_out = relayout_last(by_round, padded)
+    last = over_all(last_out)
+    own = jnp.stack(ring)
+    weights = arrange(place, own, swap(own))
+    other = swap(pair[:, 2 * padded :, :])
 
     tables = bases(cols, blocks, padded, lat_total)
     dims = (cols, blocks, bands, padded, coefs, lat_total)
-    summed = member(place, pair, innov, weights, tables, None, False, dims)
-    mine, theirs = member(place, last, innov, weights, tables, summed, True, dims)
+    summed = member(place, pair, pair, other, weights, tables, None, False, dims)
+    mine, theirs = member(place, last, pair, other, weights, tables, summed, True, dims)
     merged = (mine + swap(theirs).astype(F32)).astype(BF)
     pieces = over_all(merged)
     out = finish(place, pieces, swap(pieces), levels, cols, half, 1.0 / (ensemble - 1))

time: 184 us -> 183 us (level)
  Pallas kernels: 54.3 us -> 67.3 us
  local copies, waits for them, and re-layouts: 15.2 us -> 7.05 us
  starting transfers between devices: 37.2 us -> 30.1 us
    ppermute x6 -> x0, waiting for transfers between devices: 32.5 us -> none  [the longest x3 32.5 us: shift_x(): lax.ppermute(x, 'lon', [(z * RING + i, z * RING + (i + s) % RING) for z i...]
    ppermute x3, waiting for transfers between devices: 14 us -> 46.5 us  [shift_lat(): return lax.ppermute(x, 'lat', [(i, (i + s) % RING) for i in range(RING)])]
    ppermute x6 -> x0, starting transfers between devices: 9.94 us -> none  [the longest x3 6.56 us: shift_z(): lax.ppermute(x, 'lon', [(z * RING + i, (z + s) % RING * RING + i) for z i...]
    unnamed x38 -> x20, local copies, waits for them, and re-layouts: 15.1 us -> 5.79 us
    pallas_call x2, Pallas kernels: 30.6 us -> 36.9 us  [member(): pl.pallas_call(lambda *refs: member_kernel(*refs, first=first, final=fina...]
    all_to_all x2, starting transfers between devices: 17.2 us -> 22.9 us  [over_all(): return lax.all_to_all(x, LL, split_axis=0, concat_axis=0, tiled=True)]
    pallas_call x1, Pallas kernels: 10.2 us -> 13.9 us  [bases(): pl.pallas_call(lambda *refs: basis_kernel(*refs, cols=cols, blocks=blocks...]
    pallas_call x3, Pallas kernels: 5.61 us -> 8.57 us  [the longest x1 5 us: relayout_pair(): pl.pallas_call(lambda i, e, o: relayout_kernel(i, e, o, cols=cols, levels...]
  transfers between devices with their start and end apart: 14 -> 9, of which waited for: 6 -> 5; matrix products, arithmetic and copies ran while one was open for 1% -> 1% of each run, Pallas kernels for 18% -> 22%
where the time goes in v2:
time: 183 us; the launch traced here: 182 us
  Pallas kernels  67.3 us (37%)
  waiting for transfers between devices  50.7 us (28%)
  starting transfers between devices  30.1 us (16%)
  blocking collectives  25.3 us (14%)
  local copies, waits for them, and re-layouts  7.05 us (4%)
    ppermute x3, waiting for transfers between devices, shift_lat(): return lax.ppermute(x, 'lat', [(i, (i + s) % RING) for i in range(RING)])  46.5 us
    pallas_call x2, Pallas kernels, member(): pl.pallas_call(lambda *refs: member_kernel(*refs, first=first, final=fina...  36.9 us
    all_to_all x1, blocking collectives, over_all(): return lax.all_to_all(x, LL, split_axis=0, concat_axis=0, tiled=True)  25.3 us
    all_to_all x2, starting transfers between devices, over_all(): return lax.all_to_all(x, LL, split_axis=0, concat_axis=0, tiled=True)  22.9 us
    pallas_call x1, Pallas kernels, bases(): pl.pallas_call(lambda *refs: basis_kernel(*refs, cols=cols, blocks=blocks...  13.9 us
    unnamed x20, local copies, waits for them, and re-layouts  5.79 us
    pallas_call x1, Pallas kernels, spread(): pl.pallas_call(lambda *refs: spread_kernel(*refs, half=half, levels=level...  5.76 us
    pallas_call x1, Pallas kernels, relayout_pair(): pl.pallas_call(lambda i, e, o: relayout_kernel(i, e, o, cols=cols, levels...  5 us
  transfers between devices with their start and end apart: 9, of which 5 were waited for; matrix products, arithmetic and copies ran while one was open for 1% of the time, Pallas kernels for 22%

profile of v2, /device:TPU:1, one launch (start us, length us, event | category | flops | bytes accessed | tf_op | source)
XLA Modules:
  0.0 182.3 jit_solution(5211386600429881227)
XLA Ops:
  0.0 0.0 copy-start
  0.0 0.1 pad_add_fusion.refs_0_
  0.1 0.0 copy-start.4
  0.1 0.8 copy-done.4
  0.9 0.0 copy-start.5
  0.9 0.8 copy-done.5
  1.7 0.0 copy-start.6
  1.7 0.8 copy-done.6
  2.4 0.0 copy-start.7
  2.4 0.8 copy-done.7
  3.2 0.0 copy-start.2
  3.2 5.8 %spread.1.e = bf16[16,48,128]{2,1,0:T(8,128)(2,1)S(1)} custom-call(s32[3]{0:T(128)S(1)} %pad_add_fusion.refs_0_, s32[64,128]{1,0:T(8,128)S(1)} %copy-done.4, s32[64,128]{1,0:T(8,128)S(1)} %copy-done.5, s32[64,128]{1,0:T(8,128)S(1)} %copy-done.6, f32[64,128]{1,0:T(8,128)S(1)} %copy-done.7), custom_call_target="tpu_custom_call" | custom-call | flops 6000000000 | bytes 1048576 | tf_op jit(solution)/shard_map/spread/pallas_call | solution.py:142
  8.9 0.0 copy-start.1
  8.9 0.7 copy-done.1
  9.6 5.0 %relayout_pair.1 = bf16[64,240,128]{2,1,0:T(8,128)(2,1)} custom-call(bf16[3,4,90,16,128]{4,3,2,1,0:T(8,128)(2,1)} %bitcast.12, bf16[16,48,128]{2,1,0:T(8,128)(2,1)} %copy-done.1), custom_call_target="tpu_custom_call" | custom-call | tf_op jit(solution)/shard_map/relayout_pair/pallas_call | solution.py:76
  14.6 12.2 %all-to-all-start.1 = ((bf16[64,240,128]{2,1,0:T(8,128)(2,1)}), bf16[64,240,128]{2,1,0:T(8,128)(2,1)}, u32[]{:S(2)}, u32[]{:S(2)}) async-start(bf16[64,240,128]{2,1,0:T(8,128)(2,1)} %relayout_pair.1), calls=%async_computation.1 | async-start | bytes 7864320 | tf_op jit(solution)/shard_map/all_to_all | solution.py:35
  26.8 0.0 copy-done
  26.9 2.4 %collective-permute-start.3 = (bf16[360,256]{1,0:T(8,128)(2,1)S(1)}, bf16[360,256]{1,0:T(8,128)(2,1)S(1)}, u32[]{:S(2)}, u32[]{:S(2)}) collective-permute-start(bf16[360,256]{1,0:T(8,128)(2,1)S(1)} %fusion), channel_id=1, source_target_pairs={{0,96},{32,0},{64,32},{96,64},{1,97},{33,1},{65,33},{97,65},{2,98}... | collective-permute-start | bytes 552968 | tf_op jit(solution)/shard_map/ppermute | solution.py:39
  29.3 0.4 collective-permute-start.2
  29.7 0.7 collective-permute-start.1
  30.3 2.8 %relayout_last.1 = bf16[64,96,128]{2,1,0:T(8,128)(2,1)} custom-call(bf16[3,4,90,16,128]{4,3,2,1,0:T(8,128)(2,1)} %bitcast.13), custom_call_target="tpu_custom_call" | custom-call | tf_op jit(solution)/shard_map/relayout_last/pallas_call | solution.py:92
  33.1 41.0 %collective-permute-done.3 = bf16[360,256]{1,0:T(8,128)(2,1)S(1)} collective-permute-done((bf16[360,256]{1,0:T(8,128)(2,1)S(1)}, bf16[360,256]{1,0:T(8,128)(2,1)S(1)}, u32[]{:S(2)}, u32[]{:S(2)}) %collective-permute-start.3) | collective-permute-done | bytes 184352 | tf_op jit(solution)/shard_map/ppermute | solution.py:39
  74.1 2.2 %collective-permute-done.2 = bf16[360,256]{1,0:T(8,128)(2,1)S(1)} collective-permute-done((bf16[360,256]{1,0:T(8,128)(2,1)S(1)}, bf16[360,256]{1,0:T(8,128)(2,1)S(1)}, u32[]{:S(2)}, u32[]{:S(2)}) %collective-permute-start.2) | collective-permute-done | bytes 184352 | tf_op jit(solution)/shard_map/ppermute | solution.py:39
  76.3 3.3 %collective-permute-done.1 = bf16[360,256]{1,0:T(8,128)(2,1)S(1)} collective-permute-done((bf16[360,256]{1,0:T(8,128)(2,1)S(1)}, bf16[360,256]{1,0:T(8,128)(2,1)S(1)}, u32[]{:S(2)}, u32[]{:S(2)}) %collective-permute-start.1) | collective-permute-done | bytes 184352 | tf_op jit(solution)/shard_map/ppermute | solution.py:39
  79.6 0.1 pad_maximum_fusion.refs_1_
  79.7 1.4 collective-permute-start.4
  81.1 0.0 all-to-all-done.1.refs_1_.refs_2_
  81.1 10.8 %all-to-all-start = ((bf16[64,96,128]{2,1,0:T(8,128)(2,1)}), bf16[64,96,128]{2,1,0:T(8,128)(2,1)}, u32[]{:S(2)}, u32[]{:S(2)}) async-start(bf16[64,96,128]{2,1,0:T(8,128)(2,1)} %relayout_last.1), calls=%async_computation | async-start | bytes 3145728 | tf_op jit(solution)/shard_map/all_to_all | solution.py:35
  91.9 1.2 slice.4
  93.1 0.4 collective-permute-start
  93.5 13.9 %bases.1 = (bf16[1536,1536]{1,0:T(8,128)(2,1)}, bf16[1536,1536]{1,0:T(8,128)(2,1)}, bf16[512,512]{1,0:T(8,128)(2,1)}, bf16[512,512]{1,0:T(8,128)(2,1)}) custom-call(), custom_call_target="tpu_custom_call" | custom-call | flops 12000000000 | bytes 1048576 | tf_op jit(solution)/shard_map/bases/pallas_call | solution.py:226
  107.4 0.0 collective-permute-done.4.refs_2_
  107.4 0.0 copy-done.2
  107.4 0.8 arrange.1.refs_4_
  108.2 0.0 copy-start.8
  108.2 1.1 copy-done.8
  109.4 0.0 collective-permute-done.refs_3_
  109.4 0.0 copy-start.9
  109.4 0.9 copy-done.9
  110.3 22.8 %member_pair.1.refs_9_ = f32[64,96,128]{2,1,0:T(8,128)} custom-call(s32[3]{0:T(128)} %copy-done.2, bf16[64,240,128]{2,1,0:T(8,128)(2,1)} %all-to-all-done.1.refs_1_.refs_2_, bf16[64,240,128]{2,1,0:T(8,128)(2,1)} %all-to-all-done.1.refs_1_.refs_2_, bf16[64,48,128]{2,1,0:T(8,128)(2,1)} %copy-done.9, bf16[4,1440,128]{2,1,0:T(8,128)(2,1)} %copy-done.8, ...), custom_call_target="tpu_custom_call" | custom-call | flops 12000000000 | bytes 1048576 | tf_op jit(solution)/shard_map/member_pair/pallas_call | solution.py:377
  133.1 0.0 all-to-all-done.refs_1_
  133.1 14.1 %member_last.1 = (f32[64,48,128]{2,1,0:T(8,128)}, bf16[64,48,128]{2,1,0:T(8,128)(2,1)}) custom-call(s32[3]{0:T(128)} %copy-done.2, bf16[64,96,128]{2,1,0:T(8,128)(2,1)} %all-to-all-done.refs_1_, bf16[64,240,128]{2,1,0:T(8,128)(2,1)} %all-to-all-done.1.refs_1_.refs_2_, bf16[64,48,128]{2,1,0:T(8,128)(2,1)} %copy-done.9, bf16[4,1440,128]{2,1,0:T(8,128)(2,1)} %copy-done.8, ...), custom_call_target="tpu_custom_call" | custom-call | flops 6000000000 | bytes 1048576 | tf_op jit(solution)/shard_map/member_last/pallas_call | solution.py:377
  147.2 0.3 collective-permute-start.5
  147.5 2.3 %collective-permute-done.5 = bf16[64,48,128]{2,1,0:T(8,128)(2,1)S(1)} collective-permute-done((bf16[64,48,128]{2,1,0:T(8,128)(2,1)}, bf16[64,48,128]{2,1,0:T(8,128)(2,1)S(1)}, u32[]{:S(2)}, u32[]{:S(2)}) %collective-permute-start.5) | collective-permute-done | bytes 786464 | tf_op jit(solution)/shard_map/ppermute | solution.py:43
  149.8 1.6 add_convert_fusion
  151.4 0.0 copy-start.3
  151.4 25.3 %all_to_all.15.refs_1_ = bf16[64,48,128]{2,1,0:T(8,128)(2,1)S(1)} all-to-all(bf16[64,48,128]{2,1,0:T(8,128)(2,1)S(1)} %add_convert_fusion), channel_id=1, replica_groups=mesh['lat'=4,'lon'=16,'mem'=2] {'lat','lon'}, dimensions={0} | all-to-all | bytes 1572864 | tf_op jit(solution)/shard_map/all_to_all | solution.py:35
  176.7 1.6 collective-permute-start.6
  178.3 1.9 %collective-permute-done.6.refs_2_ = bf16[64,48,128]{2,1,0:T(8,128)(2,1)S(1)} collective-permute-done((bf16[64,48,128]{2,1,0:T(8,128)(2,1)S(1)}, bf16[64,48,128]{2,1,0:T(8,128)(2,1)S(1)}, u32[]{:S(2)}, u32[]{:S(2)}) %collective-permute-start.6) | collective-permute-done | bytes 786464 | tf_op jit(solution)/shard_map/ppermute | solution.py:43
  180.2 0.0 copy-done.3
  180.2 2.1 %finish.1 = f32[90,16,128]{2,1,0:T(8,128)} custom-call(s32[3]{0:T(128)S(1)} %copy-done.3, bf16[64,48,128]{2,1,0:T(8,128)(2,1)S(1)} %all_to_all.15.refs_1_, bf16[64,48,128]{2,1,0:T(8,128)(2,1)S(1)} %collective-permute-done.6.refs_2_), custom_call_target="tpu_custom_call" | custom-call | tf_op jit(solution)/shard_map/finish/pallas_call | solution.py:404
  (2 shorter events, 0.1 us)
Async XLA Ops:
  0.0 26.8 %copy-start = (f32[1,360,512]{2,1,0:T(8,128)S(1)}, f32[1,360,512]{2,1,0:T(8,128)}, u32[]{:S(2)}) copy-start(f32[1,360,512]{2,1,0:T(8,128)} %param.7) | copy-start | bytes 2211844
  0.1 0.8 copy-start.4
  0.9 0.8 copy-start.5
  1.7 0.8 copy-start.6
  2.4 0.8 copy-start.7
  3.2 104.3 %copy-start.2 = (s32[3]{0:T(128)}, s32[3]{0:T(128)S(1)}, u32[]{:S(2)}) copy-start(s32[3]{0:T(128)S(1)} %pad_add_fusion.refs_0_) | copy-start | bytes 40
  8.9 0.7 copy-start.1
  14.6 66.5 %all-to-all-start.1 = ((bf16[64,240,128]{2,1,0:T(8,128)(2,1)}), bf16[64,240,128]{2,1,0:T(8,128)(2,1)}, u32[]{:S(2)}, u32[]{:S(2)}) async-start(bf16[64,240,128]{2,1,0:T(8,128)(2,1)} %relayout_pair.1), calls=%async_computation.1 | async-start | bytes 7864320 | tf_op jit(solution)/shard_map/all_to_all | solution.py:35
  26.9 47.2 %collective-permute-start.3 = (bf16[360,256]{1,0:T(8,128)(2,1)S(1)}, bf16[360,256]{1,0:T(8,128)(2,1)S(1)}, u32[]{:S(2)}, u32[]{:S(2)}) collective-permute-start(bf16[360,256]{1,0:T(8,128)(2,1)S(1)} %fusion), channel_id=1, source_target_pairs={{0,96},{32,0},{64,32},{96,64},{1,97},{33,1},{65,33},{97,65},{2,98}... | collective-permute-start | bytes 552968 | tf_op jit(solution)/shard_map/ppermute | solution.py:39
  29.3 47.0 %collective-permute-start.2 = (bf16[360,256]{1,0:T(8,128)(2,1)S(1)}, bf16[360,256]{1,0:T(8,128)(2,1)S(1)}, u32[]{:S(2)}, u32[]{:S(2)}) collective-permute-start(bf16[360,256]{1,0:T(8,128)(2,1)S(1)} %fusion), channel_id=1, source_target_pairs={{0,64},{32,96},{64,0},{96,32},{1,65},{33,97},{65,1},{97,33},{2,66}... | collective-permute-start | bytes 552968 | tf_op jit(solution)/shard_map/ppermute | solution.py:39
  29.7 49.9 %collective-permute-start.1 = (bf16[360,256]{1,0:T(8,128)(2,1)S(1)}, bf16[360,256]{1,0:T(8,128)(2,1)S(1)}, u32[]{:S(2)}, u32[]{:S(2)}) collective-permute-start(bf16[360,256]{1,0:T(8,128)(2,1)S(1)} %fusion), channel_id=1, source_target_pairs={{0,32},{32,64},{64,96},{96,0},{1,33},{33,65},{65,97},{97,1},{2,34}... | collective-permute-start | bytes 552968 | tf_op jit(solution)/shard_map/ppermute | solution.py:39
  79.7 27.7 %collective-permute-start.4 = (bf16[4,360,256]{2,1,0:T(8,128)(2,1)S(1)}, bf16[4,360,256]{2,1,0:T(8,128)(2,1)S(1)}, u32[]{:S(2)}, u32[]{:S(2)}) collective-permute-start(bf16[4,360,256]{2,1,0:T(8,128)(2,1)S(1)} %pad_maximum_fusion.refs_1_), channel_id=1, source_target_pairs={{0,1},{1,0},{2,3},{3,2},{4,5},{5,4},{6,7},{7,6},{8,9},{9,8},{10,11... | collective-permute-start | bytes 2211848 | tf_op jit(solution)/shard_map/ppermute | solution.py:43
  81.1 51.9 %all-to-all-start = ((bf16[64,96,128]{2,1,0:T(8,128)(2,1)}), bf16[64,96,128]{2,1,0:T(8,128)(2,1)}, u32[]{:S(2)}, u32[]{:S(2)}) async-start(bf16[64,96,128]{2,1,0:T(8,128)(2,1)} %relayout_last.1), calls=%async_computation | async-start | bytes 3145728 | tf_op jit(solution)/shard_map/all_to_all | solution.py:35
  93.1 16.3 %collective-permute-start = (bf16[64,48,128]{2,1,0:T(8,128)(2,1)S(1)}, bf16[64,48,128]{2,1,0:T(8,128)(2,1)S(1)}, u32[]{:S(2)}, u32[]{:S(2)}) collective-permute-start(bf16[64,48,128]{2,1,0:T(8,128)(2,1)S(1)} %slice.4), channel_id=1, source_target_pairs={{0,1},{1,0},{2,3},{3,2},{4,5},{5,4},{6,7},{7,6},{8,9},{9,8},{10,11... | collective-permute-start | bytes 2359304 | tf_op jit(solution)/shard_map/ppermute | solution.py:43
  108.2 1.1 copy-start.8
  109.4 0.9 copy-start.9
  147.2 2.6 %collective-permute-start.5 = (bf16[64,48,128]{2,1,0:T(8,128)(2,1)}, bf16[64,48,128]{2,1,0:T(8,128)(2,1)S(1)}, u32[]{:S(2)}, u32[]{:S(2)}) collective-permute-start(bf16[64,48,128]{2,1,0:T(8,128)(2,1)} %get-tuple-element.16), channel_id=1, source_target_pairs={{0,1},{1,0},{2,3},{3,2},{4,5},{5,4},{6,7},{7,6},{8,9},{9,8},{10,11... | collective-permute-start | bytes 2359304 | tf_op jit(solution)/shard_map/ppermute | solution.py:43
  151.4 28.8 %copy-start.3 = (s32[3]{0:T(128)S(1)}, s32[3]{0:T(128)}, u32[]{:S(2)}) copy-start(s32[3]{0:T(128)} %copy-done.2) | copy-start | bytes 40
  176.7 3.5 %collective-permute-start.6 = (bf16[64,48,128]{2,1,0:T(8,128)(2,1)S(1)}, bf16[64,48,128]{2,1,0:T(8,128)(2,1)S(1)}, u32[]{:S(2)}, u32[]{:S(2)}) collective-permute-start(bf16[64,48,128]{2,1,0:T(8,128)(2,1)S(1)} %all_to_all.15.refs_1_), channel_id=1, source_target_pairs={{0,1},{1,0},{2,3},{3,2},{4,5},{5,4},{6,7},{7,6},{8,9},{9,8},{10,11... | collective-permute-start | bytes 2359304 | tf_op jit(solution)/shard_map/ppermute | solution.py:43
